TPU v7x, 32 devices: a whole 2x2x4 slice. The times are simulated.
32 devices in a mesh: dp: 16 (over z, y, x), tensor: 2 (over core).
Axes of the slice: x: 2, y: 2, z: 4, core: 2. Of those that a mesh axis runs over, the one named last changes fastest.
Arguments:
- tokens: bfloat16 [16384, 768], P('dp'), may hold values from -6 to 6
- memory: bfloat16 [16384, 768], P('dp'), may hold values from -6 to 6
- segment: int32 [16384], P('dp'), may hold values from 0 to 3, as said below
- cotangent: bfloat16 [16384, 768], P('dp'), may hold values from -6 to 6
- self_query: bfloat16 [768, 768], P(None, 'tensor'), may hold values from -0.21875 to 0.21875
- self_query_bias: bfloat16 [768], P('tensor'), may hold values from -3 to 3
- self_key: bfloat16 [768, 768], P(None, 'tensor'), may hold values from -0.21875 to 0.21875
- self_value: bfloat16 [768, 768], P(None, 'tensor'), may hold values from -0.21875 to 0.21875
- self_value_bias: bfloat16 [768], P('tensor'), may hold values from -3 to 3
- self_output: bfloat16 [768, 768], P('tensor'), may hold values from -0.75 to 0.75
- self_output_bias: bfloat16 [768], replicated, may hold values from -3 to 3
- cross_query: bfloat16 [768, 768], P(None, 'tensor'), may hold values from -0.21875 to 0.21875
- cross_query_bias: bfloat16 [768], P('tensor'), may hold values from -3 to 3
- cross_key: bfloat16 [768, 768], P(None, 'tensor'), may hold values from -0.21875 to 0.21875
- cross_value: bfloat16 [768, 768], P(None, 'tensor'), may hold values from -0.21875 to 0.21875
- cross_value_bias: bfloat16 [768], P('tensor'), may hold values from -3 to 3
- cross_output: bfloat16 [768, 768], P('tensor'), may hold values from -0.75 to 0.75
- cross_output_bias: bfloat16 [768], replicated, may hold values from -3 to 3
- first_gain: bfloat16 [768], replicated, may hold values from 0.5 to 1.5
- first_shift: bfloat16 [768], replicated, may hold values from -3 to 3
- second_gain: bfloat16 [768], replicated, may hold values from 0.5 to 1.5
- second_shift: bfloat16 [768], replicated, may hold values from -3 to 3
- third_gain: bfloat16 [768], replicated, may hold values from 0.5 to 1.5
- third_shift: bfloat16 [768], replicated, may hold values from -3 to 3
- inner_weight: bfloat16 [768, 3072], P(None, 'tensor'), may hold values from -0.21875 to 0.21875
- inner_bias: bfloat16 [3072], P('tensor'), may hold values from -3 to 3
- outer_weight: bfloat16 [3072, 768], P('tensor'), may hold values from -0.21875 to 0.21875
- outer_bias: bfloat16 [768], replicated, may hold values from -3 to 3
Outputs:
- output: bfloat16 [16384, 768], P('dp')
- grad_tokens: float32 [16384, 768], P(('dp', 'tensor'))
- grad_memory: float32 [16384, 768], P(('dp', 'tensor'))
- grad_self_query: float32 [768, 768], P('dp', 'tensor')
- grad_self_query_bias: float32 [768], P('tensor')
- grad_self_key: float32 [768, 768], P('dp', 'tensor')
- grad_self_value: float32 [768, 768], P('dp', 'tensor')
- grad_self_value_bias: float32 [768], P('tensor')
- grad_self_output: float32 [768, 768], P('tensor', 'dp')
- grad_self_output_bias: float32 [768], replicated
- grad_cross_query: float32 [768, 768], P('dp', 'tensor')
- grad_cross_query_bias: float32 [768], P('tensor')
- grad_cross_key: float32 [768, 768], P('dp', 'tensor')
- grad_cross_value: float32 [768, 768], P('dp', 'tensor')
- grad_cross_value_bias: float32 [768], P('tensor')
- grad_cross_output: float32 [768, 768], P('tensor', 'dp')
- grad_cross_output_bias: float32 [768], replicated
- grad_first_gain: float32 [768], replicated
- grad_first_shift: float32 [768], replicated
- grad_second_gain: float32 [768], replicated
- grad_second_shift: float32 [768], replicated
- grad_third_gain: float32 [768], replicated
- grad_third_shift: float32 [768], replicated
- grad_inner_weight: float32 [768, 3072], P('dp', 'tensor')
- grad_inner_bias: float32 [3072], P('tensor')
- grad_outer_weight: float32 [3072, 768], P('tensor', 'dp')
- grad_outer_bias: float32 [768], replicated
Inputs may be any that keep to these rules, and one draw needn't show every extreme that they name: Within each block of 1024 consecutive positions the segment is either 0 throughout (one long row) or position // 256 (four rows of 256); half of the blocks are of each kind.
All inputs are finite; a program needn't handle non-finite values.
Results may differ from a plain program's by a relative error of at most 0.028.
Values may be sent and summed in bfloat16 or wider, within the bound.
A program may use at most 256 MiB of HBM per device.

v0:
```python
from functools import partial

import jax
import jax.numpy as jnp
from jax import lax
from jax.sharding import PartitionSpec as P

HD = 64


EPSILON = 1e-05
NEGATIVE = -1e30


def normalize(hidden, gain, shift):
    center = hidden - jnp.mean(hidden, -1, keepdims=True)
    spread = jnp.mean(center * center, -1, keepdims=True)
    return center * lax.rsqrt(spread + EPSILON) * gain + shift


def project(data, weight):
    return jnp.dot(data, weight, preferred_element_type=jnp.float32)


def column_sums(values):
    return jnp.sum(values.astype(jnp.float32), 0)


def heads_of(matrix):
    return matrix.reshape(matrix.shape[0], -1, HD)


def allowed_pairs(query_segment, key_segment, start, causal):
    same = query_segment[:, None] == key_segment[None, :]
    if causal:
        query_place = start + jnp.arange(query_segment.shape[0], dtype=jnp.int32)
        key_place = jnp.arange(key_segment.shape[0], dtype=jnp.int32)
        same = same & (key_place[None, :] <= query_place[:, None])
    return same[None]


def attend_forward(queries, keys, values, segment, causal):
    length = queries.shape[0]
    block_rows = min(512, length)
    contexts = []
    totals = []
    for index in range(length // block_rows):
        start = index * block_rows
        piece = queries[start : start + block_rows]
        scores = jnp.einsum("qhe,khe->hqk", piece, keys, preferred_element_type=jnp.float32)
        scores = jnp.where(
            allowed_pairs(segment[start : start + block_rows], segment, start, causal),
            scores,
            NEGATIVE,
        )
        highest = jnp.max(scores, -1, keepdims=True)
        powers = jnp.exp(scores - highest)
        summed = jnp.sum(powers, -1, keepdims=True)
        weights = (powers / summed).astype(jnp.bfloat16)
        contexts.append(
            jnp.einsum("hqk,khe->qhe", weights, values, preferred_element_type=jnp.float32)
        )
        totals.append(highest + jnp.log(summed))
    return (jnp.concatenate(contexts, 0), jnp.concatenate(totals, 1))


def attend_backward(queries, keys, values, grad_context, totals, segment, causal):
    length = queries.shape[0]
    block_rows = min(512, length)
    grad_queries = []
    grad_keys = jnp.zeros(keys.shape, jnp.float32)
    grad_values = jnp.zeros(values.shape, jnp.float32)
    for index in range(length // block_rows):
        start = index * block_rows
        piece = queries[start : start + block_rows]
        grad_piece = grad_context[start : start + block_rows]
        scores = jnp.einsum("qhe,khe->hqk", piece, keys, preferred_element_type=jnp.float32)
        scores = jnp.where(
            allowed_pairs(segment[start : start + block_rows], segment, start, causal),
            scores,
            NEGATIVE,
        )
        probs = jnp.exp(scores - totals[:, start : start + block_rows])
        grad_probs = jnp.einsum(
            "qhe,khe->hqk", grad_piece, values, preferred_element_type=jnp.float32
        )
        row_inner = jnp.sum(grad_probs * probs, -1, keepdims=True)
        grad_scores = (probs * (grad_probs - row_inner)).astype(jnp.bfloat16)
        grad_queries.append(
            jnp.einsum("hqk,khe->qhe", grad_scores, keys, preferred_element_type=jnp.float32)
        )
        grad_keys = grad_keys + jnp.einsum(
            "hqk,qhe->khe", grad_scores, piece, preferred_element_type=jnp.float32
        )
        grad_values = grad_values + jnp.einsum(
            "hqk,qhe->khe",
            probs.astype(jnp.bfloat16),
            grad_piece,
            preferred_element_type=jnp.float32,
        )
    return (jnp.concatenate(grad_queries, 0), grad_keys, grad_values)


def on_device(
    tokens,
    memory,
    segment,
    cotangent,
    self_query,
    self_query_bias,
    self_key,
    self_value,
    self_value_bias,
    self_output,
    self_output_bias,
    cross_query,
    cross_query_bias,
    cross_key,
    cross_value,
    cross_value_bias,
    cross_output,
    cross_output_bias,
    first_gain,
    first_shift,
    second_gain,
    second_shift,
    third_gain,
    third_shift,
    inner_weight,
    inner_bias,
    outer_weight,
    outer_bias,
):
    scale = HD ** (-0.5)
    length = tokens.shape[0]
    groups = lax.axis_size("tensor")
    member = lax.axis_index("tensor")
    half = length // groups

    def rows_of(values):
        return lax.dynamic_slice_in_dim(values, member * half, half, 0)

    def spread_out(values):
        whole = jnp.zeros((values.shape[0] * groups,), jnp.float32)
        return lax.dynamic_update_slice_in_dim(whole, values, member * values.shape[0], 0)

    def own_share(values, count):
        return lax.dynamic_slice_in_dim(values, member * count, count, 0)

    queries = ((project(tokens, self_query) + self_query_bias.astype(jnp.float32)) * scale).astype(
        jnp.bfloat16
    )
    keys = project(tokens, self_key).astype(jnp.bfloat16)
    values = (project(tokens, self_value) + self_value_bias.astype(jnp.float32)).astype(
        jnp.bfloat16
    )
    self_queries = heads_of(queries)
    self_keys = heads_of(keys)
    self_values = heads_of(values)
    self_context, self_totals = attend_forward(self_queries, self_keys, self_values, segment, True)
    self_context = self_context.reshape(length, -1).astype(jnp.bfloat16)
    attended = lax.psum_scatter(
        project(self_context, self_output), "tensor", scatter_dimension=0, tiled=True
    ) + self_output_bias.astype(jnp.float32)
    first, first_back = jax.vjp(
        normalize,
        rows_of(tokens).astype(jnp.float32) + attended,
        first_gain.astype(jnp.float32),
        first_shift.astype(jnp.float32),
    )
    first_low = lax.all_gather(first.astype(jnp.bfloat16), "tensor", axis=0, tiled=True)
    queries = (
        (project(first_low, cross_query) + cross_query_bias.astype(jnp.float32)) * scale
    ).astype(jnp.bfloat16)
    keys = project(memory, cross_key).astype(jnp.bfloat16)
    values = (project(memory, cross_value) + cross_value_bias.astype(jnp.float32)).astype(
        jnp.bfloat16
    )
    cross_queries = heads_of(queries)
    cross_keys = heads_of(keys)
    cross_values = heads_of(values)
    cross_context, cross_totals = attend_forward(
        cross_queries, cross_keys, cross_values, segment, False
    )
    cross_context = cross_context.reshape(length, -1).astype(jnp.bfloat16)
    crossed = lax.psum_scatter(
        project(cross_context, cross_output).astype(jnp.bfloat16),
        "tensor",
        scatter_dimension=0,
        tiled=True,
    ).astype(jnp.float32) + cross_output_bias.astype(jnp.float32)
    second_part, second_back = jax.vjp(
        normalize,
        first + crossed,
        second_gain.astype(jnp.float32),
        second_shift.astype(jnp.float32),
    )
    second = lax.all_gather(second_part.astype(jnp.bfloat16), "tensor", axis=0, tiled=True).astype(
        second_part.dtype
    )
    second_low = second.astype(jnp.bfloat16)
    inner = project(second_low, inner_weight) + inner_bias.astype(jnp.float32)
    hidden = jax.nn.gelu(inner, approximate=False).astype(jnp.bfloat16)
    outer = lax.psum(project(hidden, outer_weight).astype(jnp.bfloat16), "tensor").astype(
        jnp.float32
    ) + outer_bias.astype(jnp.float32)
    result, third_back = jax.vjp(
        normalize, second + outer, third_gain.astype(jnp.float32), third_shift.astype(jnp.float32)
    )
    output = result.astype(jnp.bfloat16)
    grad_third, grad_third_gain, grad_third_shift = third_back(cotangent.astype(jnp.float32))
    grad_outer = grad_third.astype(jnp.bfloat16)
    grad_outer_weight = project(hidden.T, grad_outer)
    grad_outer_bias = column_sums(grad_outer)
    gelu_back = jax.vjp(partial(jax.nn.gelu, approximate=False), inner)[1]
    grad_inner = gelu_back(project(grad_outer, outer_weight.T))[0].astype(jnp.bfloat16)
    grad_inner_weight = project(second_low.T, grad_inner)
    grad_inner_bias = column_sums(grad_inner)
    grad_second = rows_of(grad_third) + lax.psum_scatter(
        project(grad_inner, inner_weight.T).astype(jnp.bfloat16),
        "tensor",
        scatter_dimension=0,
        tiled=True,
    ).astype(jnp.float32)
    grad_second_in, grad_second_gain, grad_second_shift = second_back(grad_second)
    grad_cross_rows = grad_second_in.astype(jnp.bfloat16)
    grad_cross_output_bias = column_sums(grad_cross_rows)
    grad_cross = lax.all_gather(grad_cross_rows, "tensor", axis=0, tiled=True)
    grad_cross_output = project(cross_context.T, grad_cross)
    grad_cross_context = heads_of(project(grad_cross, cross_output.T).astype(jnp.bfloat16))
    cross_grad_q, cross_grad_k, cross_grad_v = attend_backward(
        cross_queries, cross_keys, cross_values, grad_cross_context, cross_totals, segment, False
    )
    cross_grad_q = (cross_grad_q.astype(jnp.bfloat16) * scale).reshape(length, -1)
    cross_grad_k = cross_grad_k.astype(jnp.bfloat16).reshape(length, -1)
    cross_grad_v = cross_grad_v.astype(jnp.bfloat16).reshape(length, -1)
    grad_cross_query = project(first_low.T, cross_grad_q)
    grad_cross_query_bias = column_sums(cross_grad_q)
    grad_cross_key = project(memory.T, cross_grad_k)
    grad_cross_value = project(memory.T, cross_grad_v)
    grad_cross_value_bias = column_sums(cross_grad_v)
    memory_term = project(cross_grad_k, cross_key.T) + project(cross_grad_v, cross_value.T)
    grad_first = grad_second_in + lax.psum_scatter(
        project(cross_grad_q, cross_query.T).astype(jnp.bfloat16),
        "tensor",
        scatter_dimension=0,
        tiled=True,
    ).astype(jnp.float32)
    grad_first_in, grad_first_gain, grad_first_shift = first_back(grad_first)
    grad_self_rows = grad_first_in.astype(jnp.bfloat16)
    grad_self_output_bias = column_sums(grad_self_rows)
    grad_self = lax.all_gather(grad_self_rows, "tensor", axis=0, tiled=True)
    grad_self_output = project(self_context.T, grad_self)
    grad_self_context = heads_of(project(grad_self, self_output.T).astype(jnp.bfloat16))
    self_grad_q, self_grad_k, self_grad_v = attend_backward(
        self_queries, self_keys, self_values, grad_self_context, self_totals, segment, True
    )
    self_grad_q = (self_grad_q.astype(jnp.bfloat16) * scale).reshape(length, -1)
    self_grad_k = self_grad_k.astype(jnp.bfloat16).reshape(length, -1)
    self_grad_v = self_grad_v.astype(jnp.bfloat16).reshape(length, -1)
    grad_self_query = project(tokens.T, self_grad_q)
    grad_self_query_bias = column_sums(self_grad_q)
    grad_self_key = project(tokens.T, self_grad_k)
    grad_self_value = project(tokens.T, self_grad_v)
    grad_self_value_bias = column_sums(self_grad_v)
    tokens_term = (
        project(self_grad_q, self_query.T)
        + project(self_grad_k, self_key.T)
        + project(self_grad_v, self_value.T)
    )
    tokens_part, memory_part = (
        lax.psum_scatter(
            tokens_term.astype(jnp.bfloat16), "tensor", scatter_dimension=0, tiled=True
        ).astype(jnp.float32),
        lax.psum_scatter(
            memory_term.astype(jnp.bfloat16), "tensor", scatter_dimension=0, tiled=True
        ).astype(jnp.float32),
    )
    grad_tokens = tokens_part + grad_first_in
    everything = (
        lax.psum_scatter(grad_self_query, "dp", scatter_dimension=0, tiled=True),
        lax.psum_scatter(grad_self_key, "dp", scatter_dimension=0, tiled=True),
        lax.psum_scatter(grad_self_value, "dp", scatter_dimension=0, tiled=True),
        lax.psum_scatter(grad_self_output, "dp", scatter_dimension=1, tiled=True),
        lax.psum_scatter(grad_cross_query, "dp", scatter_dimension=0, tiled=True),
        lax.psum_scatter(grad_cross_key, "dp", scatter_dimension=0, tiled=True),
        lax.psum_scatter(grad_cross_value, "dp", scatter_dimension=0, tiled=True),
        lax.psum_scatter(grad_cross_output, "dp", scatter_dimension=1, tiled=True),
        lax.psum_scatter(grad_inner_weight, "dp", scatter_dimension=0, tiled=True),
        lax.psum_scatter(grad_outer_weight, "dp", scatter_dimension=1, tiled=True),
    )
    self_sums = everything[0:4]
    cross_sums = everything[4:8]
    ffn_sums = everything[8:10]
    head_columns = grad_self_query_bias.shape[0]
    unit_columns = grad_inner_bias.shape[0]
    smalls = lax.psum(
        (
            spread_out(grad_self_query_bias),
            spread_out(grad_self_value_bias),
            grad_self_output_bias,
            spread_out(grad_cross_query_bias),
            spread_out(grad_cross_value_bias),
            grad_cross_output_bias,
            grad_first_gain,
            grad_first_shift,
            grad_second_gain,
            grad_second_shift,
            grad_third_gain * 0.5,
            grad_third_shift * 0.5,
            spread_out(grad_inner_bias),
            grad_outer_bias * 0.5,
        ),
        ("dp", "tensor"),
    )
    return (
        output,
        grad_tokens,
        memory_part,
        self_sums[0],
        own_share(smalls[0], head_columns),
        self_sums[1],
        self_sums[2],
        own_share(smalls[1], head_columns),
        self_sums[3],
        smalls[2],
        cross_sums[0],
        own_share(smalls[3], head_columns),
        cross_sums[1],
        cross_sums[2],
        own_share(smalls[4], head_columns),
        cross_sums[3],
        smalls[5],
        smalls[6],
        smalls[7],
        smalls[8],
        smalls[9],
        smalls[10],
        smalls[11],
        ffn_sums[0],
        own_share(smalls[12], unit_columns),
        ffn_sums[1],
        smalls[13],
    )


def solution(mesh):
    return jax.shard_map(
        on_device,
        mesh=mesh,
        in_specs=(
            P("dp", None),
            P("dp", None),
            P("dp"),
            P("dp", None),
            P(None, "tensor"),
            P("tensor"),
            P(None, "tensor"),
            P(None, "tensor"),
            P("tensor"),
            P("tensor", None),
            P(),
            P(None, "tensor"),
            P("tensor"),
            P(None, "tensor"),
            P(None, "tensor"),
            P("tensor"),
            P("tensor", None),
            P(),
            P(),
            P(),
            P(),
            P(),
            P(),
            P(),
            P(None, "tensor"),
            P("tensor"),
            P("tensor", None),
            P(),
        ),
        out_specs=(
            P("dp", None),
            P(("dp", "tensor"), None),
            P(("dp", "tensor"), None),
            P("dp", "tensor"),
            P("tensor"),
            P("dp", "tensor"),
            P("dp", "tensor"),
            P("tensor"),
            P("tensor", "dp"),
            P(),
            P("dp", "tensor"),
            P("tensor"),
            P("dp", "tensor"),
            P("dp", "tensor"),
            P("tensor"),
            P("tensor", "dp"),
            P(),
            P(),
            P(),
            P(),
            P(),
            P(),
            P(),
            P("dp", "tensor"),
            P("tensor"),
            P("tensor", "dp"),
            P(),
        ),
        check_vma=False,
    )
```

profile of v0, /device:TPU:0, one launch (start us, length us, event | category | flops | bytes accessed | tf_op | source)
XLA Modules:
  0.0 1719.2 jit_solution(12354081403679182997)
XLA Ops:
  18.0 3.4 fusion
  22.8 4.1 fusion.55
  29.1 3.4 fusion.1
  33.8 4.1 fusion.56
  39.0 2.7 fusion.99
  41.8 13.9 reduce-scatter.27.cloned.1.call-done
  60.5 3.4 convolution_convert_fusion.6
  65.7 5.5 all-gather.5.cloned.1.call-done
  71.2 2.4 multiply_convert_fusion.5
  75.9 3.4 fusion.3
  80.5 4.1 fusion.58
  86.7 3.4 fusion.2
  91.4 4.1 fusion.57
  99.0 10.1 reduce-scatter.29.cloned.1.call-done
  113.8 11.2 all-gather.7.cloned.1.call-done
  124.9 18.2 %multiply_convert_fusion.4 = (bf16[1024,1536]{1,0:T(8,128)(2,1)S(1)}, f32[1024,1536]{1,0:T(8,128)}, f32[1024,1536]{1,0:T(8,128)}) fusion(f32[1536]{0:T(1024)S(1)} %convert_element_type.262, bf16[1024,768]{1,0:T(8,128)(2,1)} %all-gather.7.cloned.1.call-done, bf16[768,1536]{1,0:T(8,128)(2,1)S(1)} %copy-done), kind=kOutput, calls=%fused_computation.44 | convolution fusion | flops 2519728128 | bytes 19666944 | tf_op jit(solution)/shard_map/dot_general | solution.py:22
  144.9 3.7 convolution_convert_fusion.3
  148.7 21.6 %all-reduce.3.cloned.1.call-done = bf16[1024,768]{1,0:T(8,128)(2,1)} async-done(((bf16[1024,768]{1,0:T(8,128)(2,1)}), bf16[1024,768]{1,0:T(8,128)(2,1)}) %all-reduce.3.cloned.1.call-update) | async-done | bytes 1572880 | tf_op jit(solution)/shard_map/psum | solution.py:204
  170.3 2.6 fusion.43
  173.1 3.7 fusion.40
  176.9 2.9 fusion.41
  179.8 3.5 convert_reduce_fusion.2
  183.4 8.4 convert_reduce_fusion
  193.5 3.7 convolution_convert_fusion.2
  197.3 10.3 reduce-scatter.31.cloned.1.call-done
  207.7 3.5 multiply_reduce_fusion.5
  215.4 10.7 all-gather.9.cloned.1.call-done
  228.5 11.4 multiply_reduce_fusion.3
  241.3 6.7 multiply_convert_fusion.3
  250.7 11.2 multiply_reduce_fusion.2
  263.5 6.7 multiply_convert_fusion.2
  275.4 4.1 fusion.102
  279.5 5.4 add_convert_fusion.5
  285.0 4.4 fusion.10
  289.4 3.2 multiply_reduce_fusion.6
  298.6 7.1 convert_reduce_fusion.4
  310.4 9.7 multiply_reduce_fusion.1
  320.1 11.2 multiply_reduce_fusion
  332.8 18.0 %multiply_convert_fusion = (bf16[6,512,1024]{2,1,0:T(8,128)(2,1)}, bf16[6,512,1024]{2,1,0:T(8,128)(2,1)}) fusion(f32[6,512,1024]{2,1,0:T(8,128)} %get-tuple-element.155, f32[6,512,1024]{2,1,0:T(8,128)} %copy-done.5, f32[6,512]{1,0:T(8,128)S(1)} %get-tuple-element.154, f32[6,512]{1,0:T(8,128)S(1)} %log_add_fusion, pred[512,1024]{1,0:T(8,128)(4,1)S(1)} %copy-done.20, ...), kind=kLoop, calls=%fused_computation | loop fusion | flops 31457280 | bytes 64012288 | tf_op jit(solution)/shard_map/convert_element_type | solution.py:88
  350.8 5.0 convolution_convert_fusion.9
  355.8 4.1 fusion.100
  365.5 6.3 fusion.8
  371.8 4.0 convert_reduce_fusion.7
  379.1 3.5 fusion.105
  382.7 3.2 convolution_bitcast_fusion
  386.0 2.7 copy.73
  388.8 3.5 fusion.60
  392.4 3.3 convolution_bitcast_fusion.1
  395.8 2.8 copy.71
  398.6 6.2 fusion.106
  404.9 7.7 fusion.72
  413.7 3.5 fusion.104
  436.2 42.5 %all-reduce = (f32[768]{0:T(1024)S(1)}, f32[768]{0:T(1024)S(1)}, f32[768]{0:T(1024)}, f32[768]{0:T(1024)S(1)}, f32[768]{0:T(1024)S(1)}, /*index=5*/f32[768]{0:T(...) all-reduce(f32[768]{0:T(1024)S(1)} %dynamic_update_slice.15, ...), channel_id=1, replica_groups=mesh['dp'=16,'tensor'=2] {'dp','tensor'}, use_global_device_ids=true, to_apply=%region_33.34 | all-reduce | flops 13056 | bytes 104448 | tf_op jit(solution)/shard_map/psum | solution.py:297
  482.0 3.0 convert_add_fusion
  485.1 35.8 %reduce-scatter.43.cloned.1.call-done = f32[384,48]{0,1:T(8,128)} async-done(((f32[384,768]{0,1:T(8,128)}), f32[384,48]{0,1:T(8,128)}) %reduce-scatter.43.cloned.1.call-update) | async-done | bytes 73744 | tf_op jit(solution)/shard_map/reduce_scatter | solution.py:288
  520.8 129.4 %reduce-scatter.57.cloned.1.call-done = f32[48,384]{1,0:T(8,128)} async-done(((f32[768,384]{1,0:T(8,128)}), f32[48,384]{1,0:T(8,128)}) %reduce-scatter.57.cloned.1.call-update) | async-done | bytes 73744
  650.2 129.2 %reduce-scatter.41.cloned.1.call-done = f32[48,384]{1,0:T(8,128)} async-done(((f32[768,384]{1,0:T(8,128)}), f32[48,384]{1,0:T(8,128)}) %reduce-scatter.41.cloned.1.call-update) | async-done | bytes 73744 | tf_op jit(solution)/shard_map/reduce_scatter | solution.py:285
  779.5 129.2 %reduce-scatter.55.cloned.1.call-done = f32[48,384]{1,0:T(8,128)} async-done(((f32[768,384]{1,0:T(8,128)}), f32[48,384]{1,0:T(8,128)}) %reduce-scatter.55.cloned.1.call-update) | async-done | bytes 73744
  908.6 143.2 %reduce-scatter.45.cloned.1.call-done = f32[48,1536]{1,0:T(8,128)} async-done(((f32[768,1536]{1,0:T(8,128)}), f32[48,1536]{1,0:T(8,128)}) %reduce-scatter.45.cloned.1.call-update) | async-done | bytes 294928 | tf_op jit(solution)/shard_map/reduce_scatter | solution.py:289
  1051.8 143.0 %reduce-scatter.47.cloned.1.call-done = f32[1536,48]{0,1:T(8,128)} async-done(((f32[1536,768]{0,1:T(8,128)}), f32[1536,48]{0,1:T(8,128)}) %reduce-scatter.47.cloned.1.call-update) | async-done | bytes 294928 | tf_op jit(solution)/shard_map/reduce_scatter | solution.py:290
  1194.9 129.2 %reduce-scatter.39.cloned.1.call-done = f32[384,48]{0,1:T(8,128)} async-done(((f32[384,768]{0,1:T(8,128)}), f32[384,48]{0,1:T(8,128)}) %reduce-scatter.39.cloned.1.call-update) | async-done | bytes 73744 | tf_op jit(solution)/shard_map/reduce_scatter | solution.py:284
  1324.0 129.4 %reduce-scatter.53.cloned.1.call-done = f32[48,384]{1,0:T(8,128)} async-done(((f32[768,384]{1,0:T(8,128)}), f32[48,384]{1,0:T(8,128)}) %reduce-scatter.53.cloned.1.call-update) | async-done | bytes 73744
  1453.5 129.3 %reduce-scatter.51.cloned.1.call-done = f32[48,384]{1,0:T(8,128)} async-done(((f32[768,384]{1,0:T(8,128)}), f32[48,384]{1,0:T(8,128)}) %reduce-scatter.51.cloned.1.call-update) | async-done | bytes 73744
  1582.8 129.4 %reduce-scatter.49.cloned.1.call-done = f32[48,384]{1,0:T(8,128)} async-done(((f32[768,384]{1,0:T(8,128)}), f32[48,384]{1,0:T(8,128)}) %reduce-scatter.49.cloned.1.call-update) | async-done | bytes 73744
  (425 shorter events, 103.0 us)
Async XLA Ops:
  7.2 117.7 %copy-start = (bf16[768,1536]{1,0:T(8,128)(2,1)S(1)}, bf16[768,1536]{1,0:T(8,128)(2,1)}, u32[]{:S(2)}) copy-start(bf16[768,1536]{1,0:T(8,128)(2,1)} %param.52) | copy-start | bytes 7077892
  7.2 48.5 %reduce-scatter.27.cloned.1.call-start = ((), (), s32[]{:S(2)}) async-start(), calls=%async_computation.16 | async-start | bytes 4718592 | tf_op jit(solution)/shard_map/reduce_scatter | solution.py:162
  12.2 14.7 copy-start.30
  13.3 13.6 copy-start.25
  14.1 18.3 %copy-start.47 = (bf16[1024,384]{0,1:T(8,128)(2,1)}, bf16[1024,384]{0,1:T(8,128)(2,1)S(1)}, u32[]{:S(2)}) copy-start(bf16[1024,384]{0,1:T(8,128)(2,1)S(1)} %add_convert_fusion.10) | copy-start | bytes 2359300
  15.9 5.6 copy-start.17
  15.9 16.6 copy-start.19
  41.7 29.5 %all-gather.5.cloned.1.call-start = ((), (), s32[]{:S(2)}) async-start(), calls=%async_computation.17 | async-start | bytes 2359296 | tf_op jit(solution)/shard_map/all_gather | solution.py:171
  58.0 5.9 copy-start.90
  60.0 49.1 %reduce-scatter.29.cloned.1.call-start = ((), (), s32[]{:S(2)}) async-start(), calls=%async_computation.18 | async-start | bytes 2359296 | tf_op jit(solution)/shard_map/reduce_scatter | solution.py:186
  73.7 10.9 copy-start.36
  98.7 26.2 %all-gather.7.cloned.1.call-start = ((), (), s32[]{:S(2)}) async-start(), calls=%async_computation.19 | async-start | bytes 2359296 | tf_op jit(solution)/shard_map/all_gather | solution.py:198
  113.7 56.6 %all-reduce.3.cloned.1.call-start = ((), (), s32[]{:S(2)}) async-start(), calls=%async_computation.20 | async-start | bytes 3145728 | tf_op jit(solution)/shard_map/psum | solution.py:204
  124.9 20.0 %copy-start.115 = (bf16[1536,768]{1,0:T(8,128)(2,1)S(1)}, bf16[1536,768]{1,0:T(8,128)(2,1)}, u32[]{:S(2)}) copy-start(bf16[1536,768]{1,0:T(8,128)(2,1)} %param.54) | copy-start | bytes 7077892
  148.6 59.0 %reduce-scatter.31.cloned.1.call-start = ((), (), s32[]{:S(2)}) async-start(), calls=%async_computation.21 | async-start | bytes 2359296 | tf_op jit(solution)/shard_map/reduce_scatter | solution.py:219
  173.1 10.2 slice-start.14
  176.9 6.5 slice-start.15
  183.4 8.5 copy-start.23
  197.2 14.0 copy-start.13
  197.3 28.9 %all-gather.9.cloned.1.call-start = ((), (), s32[]{:S(2)}) async-start(), calls=%async_computation.22 | async-start | bytes 2359296 | tf_op jit(solution)/shard_map/all_gather | solution.py:228
  212.0 14.1 copy-start.119
  214.9 13.6 copy-start.50
  214.9 74.5 %reduce-scatter.33.cloned.1.call-start = ((), (), s32[]{:S(2)}) async-start(), calls=%async_computation.23 | async-start | bytes 2359296 | tf_op jit(solution)/shard_map/reduce_scatter | solution.py:243
  228.4 11.4 copy-start.43
  228.4 22.3 %copy-start.45 = (bf16[512,384]{0,1:T(8,128)(2,1)}, bf16[512,384]{0,1:T(8,128)(2,1)S(1)}, u32[]{:S(2)}) copy-start(bf16[512,384]{0,1:T(8,128)(2,1)S(1)} %get-tuple-element.126) | copy-start | bytes 1179652
  228.4 11.4 slice-start
  228.5 11.4 slice-start.1
  228.5 12.9 slice-start.2
  241.3 6.8 copy-start.28
  250.7 22.1 %copy-start.60 = (bf16[6,64,512]{2,1,0:T(8,128)(2,1)}, bf16[6,64,512]{2,1,0:T(8,128)(2,1)S(1)}, u32[]{:S(2)}) copy-start(bf16[6,64,512]{2,1,0:T(8,128)(2,1)S(1)} %convolution_convert_fusion.11) | copy-start | bytes 1179652
  250.7 11.2 slice-start.3
  250.7 11.2 slice-start.4
  250.7 12.7 slice-start.5
  275.0 33.0 %all-gather.11.cloned.1.call-start = ((), (), s32[]{:S(2)}) async-start(), calls=%async_computation.24 | async-start | bytes 2359296 | tf_op jit(solution)/shard_map/all_gather | solution.py:252
  275.3 56.0 %copy-start.78 = (f32[6,512]{1,0:T(8,128)}, f32[6,512]{1,0:T(8,128)S(1)}, u32[]{:S(2)}) copy-start(f32[6,512]{1,0:T(8,128)S(1)} %log_add_fusion) | copy-start | bytes 36868
  275.3 9.6 slice-start.6
  275.3 9.6 slice-start.7
  296.3 136.1 %reduce-scatter.37.cloned.1.call-start = ((), (), s32[]{:S(2)}) async-start(), calls=%async_computation.26 | async-start | bytes 2359296 | tf_op jit(solution)/shard_map/reduce_scatter | solution.py:275
  298.6 7.1 copy-start.69
  307.9 174.1 %reduce-scatter.35.cloned.1.call-start = ((), (), s32[]{:S(2)}) async-start(), calls=%async_computation.25 | async-start | bytes 2359296 | tf_op jit(solution)/shard_map/reduce_scatter | solution.py:272
  310.4 9.7 copy-start.20
  320.1 11.2 slice-start.9
  320.1 11.2 slice-start.10
  320.1 12.6 slice-start.11
  332.8 18.0 %copy-start.26 = (bf16[1024,384]{0,1:T(8,128)(2,1)S(1)}, bf16[1024,384]{0,1:T(8,128)(2,1)}, u32[]{:S(2)}) copy-start(bf16[1024,384]{0,1:T(8,128)(2,1)} %copy-done.25) | copy-start | bytes 2359300
  350.8 9.1 slice-start.12
  378.9 141.9 %reduce-scatter.43.cloned.1.call-start = ((), (), s32[]{:S(2)}) async-start(), calls=%async_computation.29 | async-start | bytes 1253376 | tf_op jit(solution)/shard_map/reduce_scatter | solution.py:288
  382.7 6.1 copy-start.61
  382.7 6.1 copy-start.64
  382.7 267.6 %reduce-scatter.57.cloned.1.call-start = ((), (), s32[]{:S(2)}) async-start(), calls=%async_computation.36 | async-start | bytes 1253376
  388.7 390.7 %reduce-scatter.41.cloned.1.call-start = ((), (), s32[]{:S(2)}) async-start(), calls=%async_computation.28 | async-start | bytes 1253376 | tf_op jit(solution)/shard_map/reduce_scatter | solution.py:285
  392.3 6.3 copy-start.11
  392.4 516.3 %reduce-scatter.55.cloned.1.call-start = ((), (), s32[]{:S(2)}) async-start(), calls=%async_computation.35 | async-start | bytes 1253376
  398.5 653.3 %reduce-scatter.45.cloned.1.call-start = ((), (), s32[]{:S(2)}) async-start(), calls=%async_computation.30 | async-start | bytes 5013504 | tf_op jit(solution)/shard_map/reduce_scatter | solution.py:289
  404.8 790.1 %reduce-scatter.47.cloned.1.call-start = ((), (), s32[]{:S(2)}) async-start(), calls=%async_computation.31 | async-start | bytes 5013504 | tf_op jit(solution)/shard_map/reduce_scatter | solution.py:290
  412.6 911.4 %reduce-scatter.39.cloned.1.call-start = ((), (), s32[]{:S(2)}) async-start(), calls=%async_computation.27 | async-start | bytes 1253376 | tf_op jit(solution)/shard_map/reduce_scatter | solution.py:284
  417.2 1036.2 %reduce-scatter.53.cloned.1.call-start = ((), (), s32[]{:S(2)}) async-start(), calls=%async_computation.34 | async-start | bytes 1253376
  420.9 1161.8 %reduce-scatter.51.cloned.1.call-start = ((), (), s32[]{:S(2)}) async-start(), calls=%async_computation.33 | async-start | bytes 1253376
  424.7 5.8 copy-start.62
  424.7 5.8 copy-start.65
  424.7 1287.4 %reduce-scatter.49.cloned.1.call-start = ((), (), s32[]{:S(2)}) async-start(), calls=%async_computation.32 | async-start | bytes 1253376
  427.2 8.5 copy-start.42
  428.7 53.4 %copy-start.89 = (f32[512]{0:T(512)S(1)}, f32[512]{0:T(512)}, u32[]{:S(2)}) copy-start(f32[512]{0:T(512)} %copy-done.88) | copy-start | bytes 6148
  431.4 1280.8 %copy-start.1 = (bf16[768,1536]{1,0:T(8,128)(2,1)S(1)}, bf16[768,1536]{1,0:T(8,128)(2,1)}, u32[]{:S(2)}) copy-start(bf16[768,1536]{1,0:T(8,128)(2,1)} %param.52) | copy-start | bytes 7077892
  (95 other events, 309.9 us)
Sparse Core Ops, SparseCore 0:
  41.8 13.8 reduce-scatter.26
  60.1 11.0 all-gather.4
  98.8 10.2 reduce-scatter.28
  113.8 11.0 all-gather.6
  148.7 21.5 all-reduce.2
  197.4 10.2 reduce-scatter.30
  215.0 11.0 all-gather.8
  275.1 10.2 reduce-scatter.32
  296.4 10.9 all-gather.10
  310.1 10.1 reduce-scatter.36
  379.0 10.1 reduce-scatter.34
  394.4 126.3 reduce-scatter.42
  526.2 124.0 reduce-scatter.56
  655.4 124.0 reduce-scatter.40
  784.6 123.9 reduce-scatter.54
  914.2 137.5 reduce-scatter.44
  1057.4 137.3 reduce-scatter.46
  1200.0 123.9 reduce-scatter.38
  1329.4 124.0 reduce-scatter.52
  1458.6 124.0 reduce-scatter.50
  1588.1 123.9 reduce-scatter.48
where the time goes:
time: 1720 us
  waiting for transfers between devices  1310 us (76%)
  matrix products  220 us (13%)
  other arithmetic  87.7 us (5%)
  blocking collectives  42.5 us (2%)
  local copies, waits for them, and re-layouts  39.7 us (2%)
    unnamed x26, waiting for transfers between devices  647 us
    reduce_scatter x1, waiting for transfers between devices, on_device(): lax.psum_scatter(grad_inner_weight, 'dp', scatter_dimension=0, tiled=True)  143 us
    reduce_scatter x1, waiting for transfers between devices, on_device(): lax.psum_scatter(grad_outer_weight, 'dp', scatter_dimension=1, tiled=True)  143 us
    reduce_scatter x1, waiting for transfers between devices, on_device(): lax.psum_scatter(grad_cross_query, 'dp', scatter_dimension=0, tiled=True)  129 us
    reduce_scatter x1, waiting for transfers between devices, on_device(): lax.psum_scatter(grad_self_output, 'dp', scatter_dimension=1, tiled=True)  129 us
    dot_general x30, matrix products, project(): return jnp.dot(data, weight, preferred_element_type=jnp.float32)  103 us
    dot_general x4, matrix products, attend_backward(): jnp.einsum('qhe,khe->hqk', grad_piece, values, preferred_element_type=jnp...  43.5 us
    psum x1, blocking collectives, on_device(): lax.psum((spread_out(grad_self_query_bias), spread_out(grad_self_value_bi...  42.5 us
  transfers between devices with their start and end apart: 21, of which 17 were waited for; matrix products, arithmetic and copies ran while one was open for 9% of the time, Pallas kernels for 0%

commit v1 on v0

--- a/solution.py
+++ b/solution.py
@@ -210,7 +210,6 @@
     output = result.astype(jnp.bfloat16)
     grad_third, grad_third_gain, grad_third_shift = third_back(cotangent.astype(jnp.float32))
     grad_outer = grad_third.astype(jnp.bfloat16)
-    grad_outer_weight = project(hidden.T, grad_outer)
     grad_outer_bias = column_sums(grad_outer)
     gelu_back = jax.vjp(partial(jax.nn.gelu, approximate=False), inner)[1]
     grad_inner = gelu_back(project(grad_outer, outer_weight.T))[0].astype(jnp.bfloat16)
@@ -226,7 +225,6 @@
     grad_cross_rows = grad_second_in.astype(jnp.bfloat16)
     grad_cross_output_bias = column_sums(grad_cross_rows)
     grad_cross = lax.all_gather(grad_cross_rows, "tensor", axis=0, tiled=True)
-    grad_cross_output = project(cross_context.T, grad_cross)
     grad_cross_context = heads_of(project(grad_cross, cross_output.T).astype(jnp.bfloat16))
     cross_grad_q, cross_grad_k, cross_grad_v = attend_backward(
         cross_queries, cross_keys, cross_values, grad_cross_context, cross_totals, segment, False
@@ -250,7 +248,6 @@
     grad_self_rows = grad_first_in.astype(jnp.bfloat16)
     grad_self_output_bias = column_sums(grad_self_rows)
     grad_self = lax.all_gather(grad_self_rows, "tensor", axis=0, tiled=True)
-    grad_self_output = project(self_context.T, grad_self)
     grad_self_context = heads_of(project(grad_self, self_output.T).astype(jnp.bfloat16))
     self_grad_q, self_grad_k, self_grad_v = attend_backward(
         self_queries, self_keys, self_values, grad_self_context, self_totals, segment, True
@@ -277,18 +274,33 @@
         ).astype(jnp.float32),
     )
     grad_tokens = tokens_part + grad_first_in
-    everything = (
-        lax.psum_scatter(grad_self_query, "dp", scatter_dimension=0, tiled=True),
-        lax.psum_scatter(grad_self_key, "dp", scatter_dimension=0, tiled=True),
-        lax.psum_scatter(grad_self_value, "dp", scatter_dimension=0, tiled=True),
-        lax.psum_scatter(grad_self_output, "dp", scatter_dimension=1, tiled=True),
-        lax.psum_scatter(grad_cross_query, "dp", scatter_dimension=0, tiled=True),
-        lax.psum_scatter(grad_cross_key, "dp", scatter_dimension=0, tiled=True),
-        lax.psum_scatter(grad_cross_value, "dp", scatter_dimension=0, tiled=True),
-        lax.psum_scatter(grad_cross_output, "dp", scatter_dimension=1, tiled=True),
-        lax.psum_scatter(grad_inner_weight, "dp", scatter_dimension=0, tiled=True),
-        lax.psum_scatter(grad_outer_weight, "dp", scatter_dimension=1, tiled=True),
-    )
+    grad_self_output_t = project(grad_self.T, self_context)
+    grad_cross_output_t = project(grad_cross.T, cross_context)
+    grad_outer_weight_t = project(grad_outer.T, hidden)
+    gathered = [
+        grad_self_query,
+        grad_self_key,
+        grad_self_value,
+        grad_self_output_t,
+        grad_cross_query,
+        grad_cross_key,
+        grad_cross_value,
+        grad_cross_output_t,
+        grad_inner_weight,
+        grad_outer_weight_t,
+    ]
+    widths = [piece.shape[1] for piece in gathered]
+    summed = lax.psum_scatter(
+        jnp.concatenate(gathered, 1), "dp", scatter_dimension=0, tiled=True
+    )
+    everything = []
+    offset = 0
+    for position, width in enumerate(widths):
+        piece = summed[:, offset : offset + width]
+        offset += width
+        if position in (3, 7, 9):
+            piece = piece.T
+        everything.append(piece)
     self_sums = everything[0:4]
     cross_sums = everything[4:8]
     ffn_sums = everything[8:10]

time: 1720 us -> 726 us (0.42)
  waiting for transfers between devices: 1310 us -> 314 us
    unnamed x26 -> x12, waiting for transfers between devices: 647 us -> 0.2 us
    reduce_scatter x5 -> x1, waiting for transfers between devices: 580 us -> 231 us  [on_device(): lax.psum_scatter(jnp.concatenate(gathered, 1), 'dp', scatter_dimension=0,...]
  transfers between devices with their start and end apart: 21 -> 12, of which waited for: 17 -> 8; matrix products, arithmetic and copies ran while one was open for 9% -> 21% of each run, Pallas kernels for 0% -> 0%
where the time goes in v1:
time: 726 us; the launch traced here: 722 us
  waiting for transfers between devices  314 us (43%)
  matrix products  206 us (28%)
  other arithmetic  86.4 us (12%)
  local copies, waits for them, and re-layouts  52 us (7%)
  blocking collectives  45.5 us (6%)
  between operations  16.2 us (2%)
    reduce_scatter x1, waiting for transfers between devices, on_device(): lax.psum_scatter(jnp.concatenate(gathered, 1), 'dp', scatter_dimension=0,...  231 us
    dot_general x30, matrix products, project(): return jnp.dot(data, weight, preferred_element_type=jnp.float32)  92 us
    psum x1, blocking collectives, on_device(): lax.psum((spread_out(grad_self_query_bias), spread_out(grad_self_value_bi...  45.5 us
    dot_general x4, matrix products, attend_backward(): jnp.einsum('qhe,khe->hqk', grad_piece, values, preferred_element_type=jnp...  40.5 us
    unnamed x303, local copies, waits for them, and re-layouts  32.6 us
    convert_element_type x3, other arithmetic, attend_backward(): grad_scores = (probs * (grad_probs - row_inner)).astype(jnp.bfloat16)  31 us
    dot_general x4, matrix products, attend_backward(): jnp.einsum('hqk,qhe->khe', probs.astype(jnp.bfloat16), grad_piece, prefer...  22.4 us
    psum x1, waiting for transfers between devices, on_device(): lax.psum(project(hidden, outer_weight).astype(jnp.bfloat16), 'tensor')  21.6 us
  transfers between devices with their start and end apart: 12, of which 8 were waited for; matrix products, arithmetic and copies ran while one was open for 21% of the time, Pallas kernels for 0%

profile of v1, /device:TPU:0, one launch (start us, length us, event | category | flops | bytes accessed | tf_op | source)
XLA Modules:
  0.0 722.2 jit_solution(16752860115697118109)
XLA Ops:
  9.7 2.4 multiply_convert_fusion.6
  18.2 3.4 fusion
  22.9 4.1 fusion.55
  29.2 3.4 fusion.1
  33.9 4.1 fusion.56
  39.1 2.7 fusion.97
  41.9 13.9 %reduce-scatter.8.cloned.1.call-done = f32[512,768]{1,0:T(8,128)} async-done(((f32[1024,768]{1,0:T(8,128)}), f32[512,768]{1,0:T(8,128)}) %reduce-scatter.8.cloned.1.call-update) | async-done | bytes 1572880 | tf_op jit(solution)/shard_map/reduce_scatter | solution.py:162
  60.8 3.4 convolution_convert_fusion.6
  66.0 5.3 all-gather.5.cloned.1.call-done
  71.3 2.4 multiply_convert_fusion.5
  76.0 3.4 fusion.3
  80.6 4.1 fusion.58
  86.8 3.4 fusion.2
  91.4 4.1 fusion.57
  96.6 2.2 convolution_convert_fusion.1
  99.1 10.1 %reduce-scatter.10.cloned.1.call-done = bf16[512,768]{1,0:T(8,128)(2,1)} async-done(((bf16[1024,768]{1,0:T(8,128)(2,1)}), bf16[512,768]{1,0:T(8,128)(2,1)}) %reduce-scatter.10.cloned.1.call-update) | async-done | bytes 786448 | tf_op jit(solution)/shard_map/reduce_scatter | solution.py:186
  109.1 2.2 fusion.90
  113.8 11.2 %all-gather.7.cloned.1.call-done = bf16[1024,768]{1,0:T(8,128)(2,1)} async-done(((bf16[512,768]{1,0:T(8,128)(2,1)}), bf16[1024,768]{1,0:T(8,128)(2,1)}) %all-gather.7.cloned.1.call-update) | async-done | bytes 1572880 | tf_op jit(solution)/shard_map/all_gather | solution.py:198
  125.0 18.3 %multiply_convert_fusion.4 = (bf16[1024,1536]{1,0:T(8,128)(2,1)S(1)}, f32[1024,1536]{1,0:T(8,128)}, f32[1024,1536]{1,0:T(8,128)}) fusion(f32[1536]{0:T(1024)S(1)} %convert_element_type.262, bf16[1024,768]{1,0:T(8,128)(2,1)} %all-gather.7.cloned.1.call-done, bf16[768,1536]{1,0:T(8,128)(2,1)S(1)} %copy-done), kind=kOutput, calls=%fused_computation.44 | convolution fusion | flops 2519728128 | bytes 19666944 | tf_op jit(solution)/shard_map/dot_general | solution.py:22
  144.9 3.7 convolution_convert_fusion.3
  148.7 21.6 %all-reduce.3.cloned.1.call-done = bf16[1024,768]{1,0:T(8,128)(2,1)} async-done(((bf16[1024,768]{1,0:T(8,128)(2,1)}), bf16[1024,768]{1,0:T(8,128)(2,1)}) %all-reduce.3.cloned.1.call-update) | async-done | bytes 1572880 | tf_op jit(solution)/shard_map/psum | solution.py:204
  170.3 2.6 fusion.43
  173.1 3.7 fusion.40
  176.9 3.0 fusion.41
  179.9 3.5 convert_reduce_fusion.2
  183.4 8.5 %convert_reduce_fusion = (f32[1536]{0:T(1024)}, bf16[1024,1536]{1,0:T(8,128)(2,1)S(1)}) fusion(f32[1024,1536]{1,0:T(8,128)S(1)} %bitcast.223, bf16[1536,768]{1,0:T(8,128)(2,1)S(1)} %copy-done.126, f32[1024,768]{1,0:T(8,128)S(1)} %get-tuple-element.53, f32[1024,1536]{1,0:T(8,128)} %get-tuple-element.105, f32[1536]{0:T(1024)S(1)} %convert_element_type.262), kind=kOutput, calls=%fused_computation.38 | convolution fusion | flops 2443442688 | bytes 21245952 | tf_op jit(solution)/shard_map/dot_general | solution.py:22
  193.6 3.7 convolution_convert_fusion.2
  197.4 10.3 %reduce-scatter.12.cloned.1.call-done = bf16[512,768]{1,0:T(8,128)(2,1)} async-done(((bf16[1024,768]{1,0:T(8,128)(2,1)}), bf16[512,768]{1,0:T(8,128)(2,1)}) %reduce-scatter.12.cloned.1.call-update) | async-done | bytes 786448 | tf_op jit(solution)/shard_map/reduce_scatter | solution.py:218
  207.7 3.5 multiply_reduce_fusion.5
  215.4 10.7 %all-gather.9.cloned.1.call-done = bf16[1024,768]{1,0:T(8,128)(2,1)} async-done(((bf16[512,768]{1,0:T(8,128)(2,1)}), bf16[1024,768]{1,0:T(8,128)(2,1)}) %all-gather.9.cloned.1.call-update) | async-done | bytes 1572880 | tf_op jit(solution)/shard_map/all_gather | solution.py:227
  226.2 2.2 convolution_convert_fusion.5
  228.5 11.2 %multiply_reduce_fusion.3 = (f32[6,512]{1,0:T(8,128)S(1)}, f32[6,512,1024]{2,1,0:T(8,128)}) fusion(f32[6,512,1024]{2,1,0:T(8,128)} %copy-done.2, f32[6,512]{1,0:T(8,128)S(1)} %log_add_fusion.2, pred[512,1024]{1,0:T(8,128)(4,1)S(1)} %get-tuple-element.87, bf16[512,6,64]{0,2,1:T(8,128)(2,1)S(1)} %bitcast.192, bf16[1024,6,64]{0,2,1:T(8,128)(2,1)S(1)} %bitcast.206), kind=kOutput, calls=%fused_computation.9 | convolution fusion | flops 415233024 | bytes 26894336 | tf_op jit(solution)/shard_map/qhe,khe->hqk/dot_general | solution.py:84
  241.1 6.7 multiply_convert_fusion.3
  250.5 11.2 %multiply_reduce_fusion.2 = (f32[6,512]{1,0:T(8,128)S(1)}, f32[6,512,1024]{2,1,0:T(8,128)}) fusion(f32[6,512,1024]{2,1,0:T(8,128)} %copy-done.3, f32[6,512]{1,0:T(8,128)S(1)} %log_add_fusion.1, pred[512,1024]{1,0:T(8,128)(4,1)S(1)} %get-tuple-element.94, bf16[512,6,64]{0,2,1:T(8,128)(2,1)S(1)} %bitcast.194, bf16[1024,6,64]{0,2,1:T(8,128)(2,1)S(1)} %bitcast.207), kind=kOutput, calls=%fused_computation.6 | convolution fusion | flops 415233024 | bytes 26894336 | tf_op jit(solution)/shard_map/qhe,khe->hqk/dot_general | solution.py:84
  263.2 6.7 multiply_convert_fusion.2
  272.5 2.2 convolution_convert_fusion
  275.6 5.3 fusion.100
  280.9 7.2 fusion.10
  288.1 5.1 convert_reduce_fusion.4
  293.2 3.2 multiply_reduce_fusion.6
  300.3 3.3 convolution_bitcast_fusion
  305.3 4.3 add_convert_fusion.5
  312.7 2.4 fusion.101
  315.1 2.2 add_convert_fusion.1
  317.6 2.2 convolution_convert_fusion.4
  320.0 6.5 fusion.8
  326.5 10.7 %multiply_reduce_fusion = (f32[6,512]{1,0:T(8,128)}, f32[6,512,1024]{2,1,0:T(8,128)}) fusion(f32[6,512,1024]{2,1,0:T(8,128)} %copy-done.5, f32[6,512]{1,0:T(8,128)S(1)} %copy-done.84, pred[512,1024]{1,0:T(8,128)(4,1)S(1)} %copy-done.25, bf16[512,6,64]{0,2,1:T(8,128)(2,1)S(1)} %bitcast.199, bf16[1024,6,64]{0,2,1:T(8,128)(2,1)S(1)} %bitcast.202), kind=kOutput, calls=%fused_computation.1 | convolution fusion | flops 415233024 | bytes 26894336 | tf_op jit(solution)/shard_map/qhe,khe->hqk/dot_general | solution.py:84
  337.2 7.4 %multiply_reduce_fusion.1 = (f32[6,512]{1,0:T(8,128)}, f32[6,512,1024]{2,1,0:T(8,128)}) fusion(f32[6,512,1024]{2,1,0:T(8,128)S(1)} %bitcast.165, f32[6,512]{1,0:T(8,128)S(1)} %log_add_fusion.3, pred[512,1024]{1,0:T(8,128)(4,1)S(1)} %copy-done.23, bf16[512,6,64]{0,2,1:T(8,128)(2,1)S(1)} %bitcast.196, bf16[1024,6,64]{0,2,1:T(8,128)(2,1)S(1)} %bitcast.203), kind=kOutput, calls=%fused_computation.4 | convolution fusion | flops 415233024 | bytes 26894336 | tf_op jit(solution)/shard_map/qhe,khe->hqk/dot_general | solution.py:84
  344.6 3.7 convert_reduce_fusion.7
  350.1 2.7 copy.57
  352.8 17.6 %multiply_convert_fusion = (bf16[6,512,1024]{2,1,0:T(8,128)(2,1)S(1)}, bf16[6,512,1024]{2,1,0:T(8,128)(2,1)S(1)}) fusion(f32[6,512,1024]{2,1,0:T(8,128)} %get-tuple-element.111, f32[6,512,1024]{2,1,0:T(8,128)} %copy-done.5, f32[6,512]{1,0:T(8,128)S(1)} %copy-done.90, f32[6,512]{1,0:T(8,128)S(1)} %copy-done.85, pred[512,1024]{1,0:T(8,128)(4,1)S(1)} %copy-done.25, ...), kind=kLoop, calls=%fused_computation | loop fusion | flops 31457280 | bytes 64012288 | tf_op jit(solution)/shard_map/convert_element_type | solution.py:88
  379.5 4.8 convolution_convert_fusion.8
  384.3 5.0 convolution_convert_fusion.9
  392.0 2.2 add_convert_fusion.2
  394.5 3.3 convolution_bitcast_fusion.4
  397.8 2.7 copy.55
  400.6 2.9 constant_dynamic-update-slice_fusion.4
  407.9 2.2 convolution_dynamic-update-slice_fusion.3
  415.2 4.4 convolution_dynamic-update-slice_fusion.1
  419.6 4.3 convolution_dynamic-update-slice_fusion
  425.5 2.4 convert_element_type.300
  428.7 45.5 %all-reduce = (f32[768]{0:T(1024)S(1)}, f32[768]{0:T(1024)S(1)}, f32[768]{0:T(1024)}, f32[768]{0:T(1024)S(1)}, f32[768]{0:T(1024)S(1)}, /*index=5*/f32[768]{0:T(...) all-reduce(f32[768]{0:T(1024)S(1)} %dynamic_update_slice.15, ...), channel_id=1, replica_groups=mesh['dp'=16,'tensor'=2] {'dp','tensor'}, use_global_device_ids=true, to_apply=%region_33.34 | all-reduce | flops 13056 | bytes 104448 | tf_op jit(solution)/shard_map/psum | solution.py:309
  477.5 3.1 convert_add_fusion
  480.6 230.7 %reduce-scatter.20.cloned.1.call-done = f32[48,6144]{1,0:T(8,128)} async-done(((f32[768,6144]{1,0:T(8,128)}), f32[48,6144]{1,0:T(8,128)}) %reduce-scatter.20.cloned.1.call-update) | async-done | bytes 1179664 | tf_op jit(solution)/shard_map/reduce_scatter | solution.py:293
  (426 shorter events, 89.7 us)
Async XLA Ops:
  7.2 117.8 %copy-start = (bf16[768,1536]{1,0:T(8,128)(2,1)S(1)}, bf16[768,1536]{1,0:T(8,128)(2,1)}, u32[]{:S(2)}) copy-start(bf16[768,1536]{1,0:T(8,128)(2,1)} %param.52) | copy-start | bytes 7077892
  7.2 4.9 copy-start.77
  7.2 48.6 %reduce-scatter.8.cloned.1.call-start = ((), (), s32[]{:S(2)}) async-start(), calls=%async_computation.7 | async-start | bytes 4718592 | tf_op jit(solution)/shard_map/reduce_scatter | solution.py:162
  7.3 4.9 copy-start.81
  12.2 14.9 %copy-start.35 = (bf16[512,384]{0,1:T(8,128)(2,1)}, bf16[512,384]{0,1:T(8,128)(2,1)S(1)}, u32[]{:S(2)}) copy-start(bf16[512,384]{0,1:T(8,128)(2,1)S(1)} %get-tuple-element.86) | copy-start | bytes 1179652
  13.3 13.8 %copy-start.28 = (bf16[1024,384]{0,1:T(8,128)(2,1)}, bf16[1024,384]{0,1:T(8,128)(2,1)S(1)}, u32[]{:S(2)}) copy-start(bf16[1024,384]{0,1:T(8,128)(2,1)S(1)} %convolution_convert_fusion.7) | copy-start | bytes 2359300
  14.1 18.4 %copy-start.50 = (bf16[1024,384]{0,1:T(8,128)(2,1)}, bf16[1024,384]{0,1:T(8,128)(2,1)S(1)}, u32[]{:S(2)}) copy-start(bf16[1024,384]{0,1:T(8,128)(2,1)S(1)} %add_convert_fusion.10) | copy-start | bytes 2359300
  16.0 5.6 copy-start.22
  16.0 16.6 %copy-start.24 = (pred[512,1024]{1,0:T(8,128)(4,1)}, pred[512,1024]{1,0:T(8,128)(4,1)S(1)}, u32[]{:S(2)}) copy-start(pred[512,1024]{1,0:T(8,128)(4,1)S(1)} %get-tuple-element.93) | copy-start | bytes 1572868
  18.2 4.7 copy-start.86
  21.5 5.5 copy-start.92
  29.2 4.7 copy-start.88
  33.9 5.1 copy-start.74
  41.8 29.5 %all-gather.5.cloned.1.call-start = ((), (), s32[]{:S(2)}) async-start(), calls=%async_computation.8 | async-start | bytes 2359296 | tf_op jit(solution)/shard_map/all_gather | solution.py:171
  58.1 6.1 copy-start.98
  60.1 49.0 %reduce-scatter.10.cloned.1.call-start = ((), (), s32[]{:S(2)}) async-start(), calls=%async_computation.9 | async-start | bytes 2359296 | tf_op jit(solution)/shard_map/reduce_scatter | solution.py:186
  73.8 10.9 %copy-start.41 = (bf16[512,384]{0,1:T(8,128)(2,1)}, bf16[512,384]{0,1:T(8,128)(2,1)S(1)}, u32[]{:S(2)}) copy-start(bf16[512,384]{0,1:T(8,128)(2,1)S(1)} %get-tuple-element.83) | copy-start | bytes 1179652
  91.4 5.2 copy-start.132
  98.8 26.2 %all-gather.7.cloned.1.call-start = ((), (), s32[]{:S(2)}) async-start(), calls=%async_computation.10 | async-start | bytes 2359296 | tf_op jit(solution)/shard_map/all_gather | solution.py:198
  113.7 56.6 %all-reduce.3.cloned.1.call-start = ((), (), s32[]{:S(2)}) async-start(), calls=%async_computation.11 | async-start | bytes 3145728 | tf_op jit(solution)/shard_map/psum | solution.py:204
  125.0 19.9 %copy-start.125 = (bf16[1536,768]{1,0:T(8,128)(2,1)S(1)}, bf16[1536,768]{1,0:T(8,128)(2,1)}, u32[]{:S(2)}) copy-start(bf16[1536,768]{1,0:T(8,128)(2,1)} %param.54) | copy-start | bytes 7077892
  148.6 59.1 %reduce-scatter.12.cloned.1.call-start = ((), (), s32[]{:S(2)}) async-start(), calls=%async_computation.12 | async-start | bytes 2359296 | tf_op jit(solution)/shard_map/reduce_scatter | solution.py:218
  173.1 10.2 %slice-start.12 = ((s8[6291456]{0:T(1024)(128)(4,1)}), s8[4194304]{0:T(1024)(128)(4,1)S(1)}, s32[]{:S(2)}) async-start(s8[6291456]{0:T(1024)(128)(4,1)} %bitcast.222), calls=%async_computation.31 | async-start | bytes 8388608
  176.9 6.5 slice-start.13
  183.4 8.5 %copy-start.16 = (f32[1024,768]{1,0:T(8,128)}, f32[1024,768]{1,0:T(8,128)S(1)}, u32[]{:S(2)}) copy-start(f32[1024,768]{1,0:T(8,128)S(1)} %get-tuple-element.53) | copy-start | bytes 9437188
  197.3 14.0 %copy-start.15 = (f32[512,768]{1,0:T(8,128)S(1)}, f32[512,768]{1,0:T(8,128)}, u32[]{:S(2)}) copy-start(f32[512,768]{1,0:T(8,128)} %copy-done.14) | copy-start | bytes 4718596
  197.3 28.8 %all-gather.9.cloned.1.call-start = ((), (), s32[]{:S(2)}) async-start(), calls=%async_computation.13 | async-start | bytes 2359296 | tf_op jit(solution)/shard_map/all_gather | solution.py:227
  212.0 14.1 %copy-start.133 = (bf16[384,768]{1,0:T(8,128)(2,1)S(1)}, bf16[384,768]{1,0:T(8,128)(2,1)}, u32[]{:S(2)}) copy-start(bf16[384,768]{1,0:T(8,128)(2,1)} %param.44) | copy-start | bytes 1769476
  214.9 13.6 %copy-start.53 = (bf16[1024,384]{0,1:T(8,128)(2,1)S(1)}, bf16[1024,384]{0,1:T(8,128)(2,1)}, u32[]{:S(2)}) copy-start(bf16[1024,384]{0,1:T(8,128)(2,1)} %add_convert_fusion.9) | copy-start | bytes 2359300
  214.9 78.3 %reduce-scatter.14.cloned.1.call-start = ((), (), s32[]{:S(2)}) async-start(), calls=%async_computation.14 | async-start | bytes 2359296 | tf_op jit(solution)/shard_map/reduce_scatter | solution.py:241
  228.4 11.2 %slice-start = ((s8[12582912]{0:T(1024)(128)(4,1)}), s8[4194304]{0:T(1024)(128)(4,1)S(1)}, s32[]{:S(2)}) async-start(s8[12582912]{0:T(1024)(128)(4,1)} %bitcast.158), calls=%async_computation.19 | async-start | bytes 8388608
  228.5 11.2 %slice-start.1 = ((s8[12582912]{0:T(1024)(128)(4,1)}), s8[4194304]{0:T(1024)(128)(4,1)S(1)}, s32[]{:S(2)}) async-start(s8[12582912]{0:T(1024)(128)(4,1)} %bitcast.158), calls=%async_computation.20 | async-start | bytes 8388608
  228.5 12.6 %slice-start.2 = ((s8[12582912]{0:T(1024)(128)(4,1)}), s8[4194304]{0:T(1024)(128)(4,1)S(1)}, s32[]{:S(2)}) async-start(s8[12582912]{0:T(1024)(128)(4,1)} %bitcast.158), calls=%async_computation.21 | async-start | bytes 8388608
  241.1 6.8 copy-start.31
  250.5 22.1 %copy-start.66 = (bf16[6,64,512]{2,1,0:T(8,128)(2,1)}, bf16[6,64,512]{2,1,0:T(8,128)(2,1)S(1)}, u32[]{:S(2)}) copy-start(bf16[6,64,512]{2,1,0:T(8,128)(2,1)S(1)} %convolution_convert_fusion.11) | copy-start | bytes 1179652
  250.5 11.2 %slice-start.6 = ((s8[12582912]{0:T(1024)(128)(4,1)}), s8[4194304]{0:T(1024)(128)(4,1)S(1)}, s32[]{:S(2)}) async-start(s8[12582912]{0:T(1024)(128)(4,1)} %bitcast.162), calls=%async_computation.25 | async-start | bytes 8388608
  250.5 11.2 %slice-start.7 = ((s8[12582912]{0:T(1024)(128)(4,1)}), s8[4194304]{0:T(1024)(128)(4,1)S(1)}, s32[]{:S(2)}) async-start(s8[12582912]{0:T(1024)(128)(4,1)} %bitcast.162), calls=%async_computation.26 | async-start | bytes 8388608
  250.5 12.7 %slice-start.8 = ((s8[12582912]{0:T(1024)(128)(4,1)}), s8[4194304]{0:T(1024)(128)(4,1)S(1)}, s32[]{:S(2)}) async-start(s8[12582912]{0:T(1024)(128)(4,1)} %bitcast.162), calls=%async_computation.27 | async-start | bytes 8388608
  272.5 8.4 %copy-start.68 = (bf16[6,64,512]{2,1,0:T(8,128)(2,1)}, bf16[6,64,512]{2,1,0:T(8,128)(2,1)S(1)}, u32[]{:S(2)}) copy-start(bf16[6,64,512]{2,1,0:T(8,128)(2,1)S(1)} %convolution_convert_fusion.10) | copy-start | bytes 1179652
  274.7 42.9 %all-gather.11.cloned.1.call-start = ((), (), s32[]{:S(2)}) async-start(), calls=%async_computation.15 | async-start | bytes 2359296 | tf_op jit(solution)/shard_map/all_gather | solution.py:250
  275.6 12.5 %slice-start.3 = ((s8[12582912]{0:T(1024)(128)(4,1)}), s8[4194304]{0:T(1024)(128)(4,1)S(1)}, s32[]{:S(2)}) async-start(s8[12582912]{0:T(1024)(128)(4,1)} %bitcast.160), calls=%async_computation.22 | async-start | bytes 8388608
  275.6 12.5 %slice-start.4 = ((s8[12582912]{0:T(1024)(128)(4,1)}), s8[4194304]{0:T(1024)(128)(4,1)S(1)}, s32[]{:S(2)}) async-start(s8[12582912]{0:T(1024)(128)(4,1)} %bitcast.160), calls=%async_computation.23 | async-start | bytes 8388608
  280.9 7.2 slice-start.5
  288.1 5.1 copy-start.11
  300.2 125.3 %reduce-scatter.18.cloned.1.call-start = ((), (), s32[]{:S(2)}) async-start(), calls=%async_computation.17 | async-start | bytes 2359296 | tf_op jit(solution)/shard_map/reduce_scatter | solution.py:272
  300.3 5.0 copy-start.32
  300.3 5.0 copy-start.38
  305.3 5.2 copy-start.128
  317.3 160.2 %reduce-scatter.16.cloned.1.call-start = ((), (), s32[]{:S(2)}) async-start(), calls=%async_computation.16 | async-start | bytes 2359296 | tf_op jit(solution)/shard_map/reduce_scatter | solution.py:269
  319.9 6.5 copy-start.51
  319.9 17.3 %slice-start.9 = ((s8[12582912]{0:T(1024)(128)(4,1)}), s8[4194304]{0:T(1024)(128)(4,1)S(1)}, s32[]{:S(2)}) async-start(s8[12582912]{0:T(1024)(128)(4,1)} %bitcast.164), calls=%async_computation.28 | async-start | bytes 8388608
  319.9 17.2 %slice-start.10 = ((s8[12582912]{0:T(1024)(128)(4,1)}), s8[4194304]{0:T(1024)(128)(4,1)S(1)}, s32[]{:S(2)}) async-start(s8[12582912]{0:T(1024)(128)(4,1)} %bitcast.164), calls=%async_computation.29 | async-start | bytes 8388608
  326.5 10.7 %slice-start.11 = ((s8[12582912]{0:T(1024)(128)(4,1)}), s8[4194304]{0:T(1024)(128)(4,1)S(1)}, s32[]{:S(2)}) async-start(s8[12582912]{0:T(1024)(128)(4,1)} %bitcast.164), calls=%async_computation.30 | async-start | bytes 8388608
  326.5 10.7 %copy-start.23 = (pred[512,1024]{1,0:T(8,128)(4,1)S(1)}, pred[512,1024]{1,0:T(8,128)(4,1)}, u32[]{:S(2)}) copy-start(pred[512,1024]{1,0:T(8,128)(4,1)} %copy-done.22) | copy-start | bytes 1572868
  352.8 17.6 %copy-start.40 = (bf16[512,384]{0,1:T(8,128)(2,1)S(1)}, bf16[512,384]{0,1:T(8,128)(2,1)}, u32[]{:S(2)}) copy-start(bf16[512,384]{0,1:T(8,128)(2,1)} %copy-done.39) | copy-start | bytes 1179652
  384.3 10.2 %copy-start.46 = (bf16[6,64,512]{2,1,0:T(8,128)(2,1)}, bf16[6,64,512]{2,1,0:T(8,128)(2,1)S(1)}, u32[]{:S(2)}) copy-start(bf16[6,64,512]{2,1,0:T(8,128)(2,1)S(1)} %convolution_convert_fusion.8) | copy-start | bytes 1179652
  384.3 5.0 copy-start.76
  394.3 317.0 %reduce-scatter.20.cloned.1.call-start = ((), (), s32[]{:S(2)}) async-start(), calls=%async_computation.18 | async-start | bytes 20054016 | tf_op jit(solution)/shard_map/reduce_scatter | solution.py:293
  397.8 6.8 copy-start.34
  400.6 5.2 copy-start.64
  400.6 5.2 copy-start.131
  423.9 4.7 copy-start.100
  424.0 53.5 %copy-start.97 = (f32[512]{0:T(512)S(1)}, f32[512]{0:T(512)}, u32[]{:S(2)}) copy-start(f32[512]{0:T(512)} %copy-done.96) | copy-start | bytes 6148
  476.8 238.3 %copy-start.1 = (bf16[768,1536]{1,0:T(8,128)(2,1)S(1)}, bf16[768,1536]{1,0:T(8,128)(2,1)}, u32[]{:S(2)}) copy-start(bf16[768,1536]{1,0:T(8,128)(2,1)} %param.52) | copy-start | bytes 7077892
  (97 other events, 278.8 us)
Sparse Core Ops, SparseCore 0:
  41.9 13.8 reduce-scatter.7
  60.2 11.0 all-gather.4
  98.9 10.2 reduce-scatter.9
  113.9 11.0 all-gather.6
  148.8 21.5 all-reduce.2
  197.4 10.2 reduce-scatter.11
  215.0 11.0 all-gather.8
  274.8 10.2 reduce-scatter.13
  300.3 10.9 all-gather.10
  317.4 10.2 reduce-scatter.17
  394.4 10.2 reduce-scatter.15
  424.0 287.2 reduce-scatter.19

commit v2 on v1

--- a/solution.py
+++ b/solution.py
@@ -147,6 +147,35 @@
     def own_share(values, count):
         return lax.dynamic_slice_in_dim(values, member * count, count, 0)
 
+    def swap(values):
+        return lax.ppermute(values, "tensor", [(0, 1), (1, 0)])
+
+    def gather_rows(values):
+        if groups != 2:
+            return lax.all_gather(values, "tensor", axis=0, tiled=True)
+        other = swap(values)
+        lead = member == 0
+        return jnp.concatenate(
+            [jnp.where(lead, values, other), jnp.where(lead, other, values)], 0
+        )
+
+    def scatter_rows(values):
+        if groups != 2:
+            return lax.psum_scatter(
+                values, "tensor", scatter_dimension=0, tiled=True
+            ).astype(jnp.float32)
+        top = values[:half]
+        bottom = values[half:]
+        lead = member == 0
+        keep = jnp.where(lead, top, bottom)
+        send = jnp.where(lead, bottom, top)
+        return keep.astype(jnp.float32) + swap(send).astype(jnp.float32)
+
+    def sum_pair(values):
+        if groups != 2:
+            return lax.psum(values, "tensor").astype(jnp.float32)
+        return values.astype(jnp.float32) + swap(values).astype(jnp.float32)
+
     queries = ((project(tokens, self_query) + self_query_bias.astype(jnp.float32)) * scale).astype(
         jnp.bfloat16
     )
@@ -159,16 +188,16 @@
     self_values = heads_of(values)
     self_context, self_totals = attend_forward(self_queries, self_keys, self_values, segment, True)
     self_context = self_context.reshape(length, -1).astype(jnp.bfloat16)
-    attended = lax.psum_scatter(
-        project(self_context, self_output), "tensor", scatter_dimension=0, tiled=True
-    ) + self_output_bias.astype(jnp.float32)
+    attended = scatter_rows(project(self_context, self_output)) + self_output_bias.astype(
+        jnp.float32
+    )
     first, first_back = jax.vjp(
         normalize,
         rows_of(tokens).astype(jnp.float32) + attended,
         first_gain.astype(jnp.float32),
         first_shift.astype(jnp.float32),
     )
-    first_low = lax.all_gather(first.astype(jnp.bfloat16), "tensor", axis=0, tiled=True)
+    first_low = gather_rows(first.astype(jnp.bfloat16))
     queries = (
         (project(first_low, cross_query) + cross_query_bias.astype(jnp.float32)) * scale
     ).astype(jnp.bfloat16)
@@ -183,27 +212,22 @@
         cross_queries, cross_keys, cross_values, segment, False
     )
     cross_context = cross_context.reshape(length, -1).astype(jnp.bfloat16)
-    crossed = lax.psum_scatter(
-        project(cross_context, cross_output).astype(jnp.bfloat16),
-        "tensor",
-        scatter_dimension=0,
-        tiled=True,
-    ).astype(jnp.float32) + cross_output_bias.astype(jnp.float32)
+    crossed = scatter_rows(
+        project(cross_context, cross_output).astype(jnp.bfloat16)
+    ) + cross_output_bias.astype(jnp.float32)
     second_part, second_back = jax.vjp(
         normalize,
         first + crossed,
         second_gain.astype(jnp.float32),
         second_shift.astype(jnp.float32),
     )
-    second = lax.all_gather(second_part.astype(jnp.bfloat16), "tensor", axis=0, tiled=True).astype(
-        second_part.dtype
-    )
+    second = gather_rows(second_part.astype(jnp.bfloat16)).astype(second_part.dtype)
     second_low = second.astype(jnp.bfloat16)
     inner = project(second_low, inner_weight) + inner_bias.astype(jnp.float32)
     hidden = jax.nn.gelu(inner, approximate=False).astype(jnp.bfloat16)
-    outer = lax.psum(project(hidden, outer_weight).astype(jnp.bfloat16), "tensor").astype(
+    outer = sum_pair(project(hidden, outer_weight).astype(jnp.bfloat16)) + outer_bias.astype(
         jnp.float32
-    ) + outer_bias.astype(jnp.float32)
+    )
     result, third_back = jax.vjp(
         normalize, second + outer, third_gain.astype(jnp.float32), third_shift.astype(jnp.float32)
     )
@@ -215,16 +239,13 @@
     grad_inner = gelu_back(project(grad_outer, outer_weight.T))[0].astype(jnp.bfloat16)
     grad_inner_weight = project(second_low.T, grad_inner)
     grad_inner_bias = column_sums(grad_inner)
-    grad_second = rows_of(grad_third) + lax.psum_scatter(
-        project(grad_inner, inner_weight.T).astype(jnp.bfloat16),
-        "tensor",
-        scatter_dimension=0,
-        tiled=True,
-    ).astype(jnp.float32)
+    grad_second = rows_of(grad_third) + scatter_rows(
+        project(grad_inner, inner_weight.T).astype(jnp.bfloat16)
+    )
     grad_second_in, grad_second_gain, grad_second_shift = second_back(grad_second)
     grad_cross_rows = grad_second_in.astype(jnp.bfloat16)
     grad_cross_output_bias = column_sums(grad_cross_rows)
-    grad_cross = lax.all_gather(grad_cross_rows, "tensor", axis=0, tiled=True)
+    grad_cross = gather_rows(grad_cross_rows)
     grad_cross_context = heads_of(project(grad_cross, cross_output.T).astype(jnp.bfloat16))
     cross_grad_q, cross_grad_k, cross_grad_v = attend_backward(
         cross_queries, cross_keys, cross_values, grad_cross_context, cross_totals, segment, False
@@ -238,16 +259,13 @@
     grad_cross_value = project(memory.T, cross_grad_v)
     grad_cross_value_bias = column_sums(cross_grad_v)
     memory_term = project(cross_grad_k, cross_key.T) + project(cross_grad_v, cross_value.T)
-    grad_first = grad_second_in + lax.psum_scatter(
-        project(cross_grad_q, cross_query.T).astype(jnp.bfloat16),
-        "tensor",
-        scatter_dimension=0,
-        tiled=True,
-    ).astype(jnp.float32)
+    grad_first = grad_second_in + scatter_rows(
+        project(cross_grad_q, cross_query.T).astype(jnp.bfloat16)
+    )
     grad_first_in, grad_first_gain, grad_first_shift = first_back(grad_first)
     grad_self_rows = grad_first_in.astype(jnp.bfloat16)
     grad_self_output_bias = column_sums(grad_self_rows)
-    grad_self = lax.all_gather(grad_self_rows, "tensor", axis=0, tiled=True)
+    grad_self = gather_rows(grad_self_rows)
     grad_self_context = heads_of(project(grad_self, self_output.T).astype(jnp.bfloat16))
     self_grad_q, self_grad_k, self_grad_v = attend_backward(
         self_queries, self_keys, self_values, grad_self_context, self_totals, segment, True
@@ -265,14 +283,8 @@
         + project(self_grad_k, self_key.T)
         + project(self_grad_v, self_value.T)
     )
-    tokens_part, memory_part = (
-        lax.psum_scatter(
-            tokens_term.astype(jnp.bfloat16), "tensor", scatter_dimension=0, tiled=True
-        ).astype(jnp.float32),
-        lax.psum_scatter(
-            memory_term.astype(jnp.bfloat16), "tensor", scatter_dimension=0, tiled=True
-        ).astype(jnp.float32),
-    )
+    tokens_part = scatter_rows(tokens_term.astype(jnp.bfloat16))
+    memory_part = scatter_rows(memory_term.astype(jnp.bfloat16))
     grad_tokens = tokens_part + grad_first_in
     grad_self_output_t = project(grad_self.T, self_context)
     grad_cross_output_t = project(grad_cross.T, cross_context)

time: 726 us -> 630 us (0.87)
  waiting for transfers between devices: 314 us -> 233 us
  matrix products: 206 us -> 188 us
  local copies, waits for them, and re-layouts: 52 us -> 43.5 us
    reduce_scatter x6 -> x0, waiting for transfers between devices: 34.3 us -> none  [the longest x1 13.9 us: on_device(): lax.psum_scatter(project(self_context, self_output), 'tensor', scatter_di...]
    all_gather x4 -> x0, waiting for transfers between devices: 27.3 us -> none  [the longest x1 11.2 us: on_device(): lax.all_gather(second_part.astype(jnp.bfloat16), 'tensor', axis=0, tiled=...]
    psum x1 -> x0, waiting for transfers between devices: 21.6 us -> none  [on_device(): lax.psum(project(hidden, outer_weight).astype(jnp.bfloat16), 'tensor')]
    ppermute x0 -> x11, waiting for transfers between devices: none -> 13.3 us  [swap(): return lax.ppermute(values, 'tensor', [(0, 1), (1, 0)])]
    dot_general x30, matrix products: 92 us -> 79.1 us  [project(): return jnp.dot(data, weight, preferred_element_type=jnp.float32)]
    reduce_scatter x1, waiting for transfers between devices: 231 us -> 220 us  [on_device(): lax.psum_scatter(jnp.concatenate(gathered, 1), 'dp', scatter_dimension=0,...]
    unnamed x303 -> x307, local copies, waits for them, and re-layouts: 32.6 us -> 24.1 us
  transfers between devices with their start and end apart: 12 -> 12, of which waited for: 8 -> 7; matrix products, arithmetic and copies ran while one was open for 21% -> 6% of each run, Pallas kernels for 0% -> 0%
where the time goes in v2:
time: 630 us; the launch traced here: 621 us
  waiting for transfers between devices  233 us (37%)
  matrix products  188 us (30%)
  other arithmetic  88.6 us (14%)
  blocking collectives  46.4 us (7%)
  local copies, waits for them, and re-layouts  43.5 us (7%)
  between operations  16.3 us (3%)
    reduce_scatter x1, waiting for transfers between devices, on_device(): lax.psum_scatter(jnp.concatenate(gathered, 1), 'dp', scatter_dimension=0,...  220 us
    dot_general x30, matrix products, project(): return jnp.dot(data, weight, preferred_element_type=jnp.float32)  79.1 us
    psum x1, blocking collectives, on_device(): lax.psum((spread_out(grad_self_query_bias), spread_out(grad_self_value_bi...  46.4 us
    convert_element_type x3, other arithmetic, attend_backward(): grad_scores = (probs * (grad_probs - row_inner)).astype(jnp.bfloat16)  34.5 us
    dot_general x4, matrix products, attend_backward(): jnp.einsum('qhe,khe->hqk', grad_piece, values, preferred_element_type=jnp...  33.9 us
    unnamed x307, local copies, waits for them, and re-layouts  24.1 us
    dot_general x4, matrix products, attend_backward(): jnp.einsum('hqk,qhe->khe', probs.astype(jnp.bfloat16), grad_piece, prefer...  21.2 us
    dot_general x4, matrix products, attend_forward(): jnp.einsum('hqk,khe->qhe', weights, values, preferred_element_type=jnp.fl...  18 us
  transfers between devices with their start and end apart: 12, of which 7 were waited for; matrix products, arithmetic and copies ran while one was open for 6% of the time, Pallas kernels for 0%

profile of v2, /device:TPU:0, one launch (start us, length us, event | category | flops | bytes accessed | tf_op | source)
XLA Modules:
  0.0 620.6 jit_solution(12197545219358011029)
XLA Ops:
  9.7 2.4 multiply_convert_fusion.6
  15.7 2.1 select_reduce_fusion.3
  17.9 3.4 fusion
  22.6 4.7 fusion.53
  27.4 2.1 select_reduce_fusion.2
  29.5 3.4 fusion.1
  34.1 4.9 fusion.54
  41.1 2.1 fusion.102
  46.8 3.3 collective-permute-done
  50.1 2.9 fusion.96
  58.7 2.1 select_reduce_fusion
  60.9 3.4 fusion.3
  65.5 4.2 fusion.56
  69.7 2.1 select_reduce_fusion.1
  71.8 3.9 fusion.2
  75.7 4.2 fusion.55
  82.5 1.9 collective-permute-done.2
  86.3 1.9 collective-permute-done.3
  88.8 17.7 %multiply_convert_fusion.4 = (bf16[1024,1536]{1,0:T(8,128)(2,1)S(1)}, f32[1024,1536]{1,0:T(8,128)}, f32[1024,1536]{1,0:T(8,128)}) fusion(f32[1536]{0:T(1024)S(1)} %convert_element_type.281, bf16[768,1536]{1,0:T(8,128)(2,1)S(1)} %copy-done, bf16[512,768]{1,0:T(8,128)(2,1)S(1)} %get-tuple-element.78, bf16[512,768]{1,0:T(8,128)(2,1)S(1)} %get-tuple-element.77), kind=kOutput, calls=%fused_computation.44 | convolution fusion | flops 2522873856 | bytes 19666944 | tf_op jit(solution)/shard_map/dot_general | solution.py:22
  106.5 2.6 convolution_convert_fusion.3
  109.6 3.0 collective-permute-done.4
  115.2 2.6 fusion.41
  117.8 3.0 convert_reduce_fusion.2
  120.8 11.1 %convert_reduce_fusion = (f32[1536]{0:T(1024)}, bf16[1024,1536]{1,0:T(8,128)(2,1)}) fusion(f32[1024,1536]{1,0:T(8,128)} %get-tuple-element.67, bf16[1536,768]{1,0:T(8,128)(2,1)} %param.54, f32[1024,768]{1,0:T(8,128)S(1)} %get-tuple-element.53, f32[1024,1536]{1,0:T(8,128)} %get-tuple-element.117, f32[1536]{0:T(1024)S(1)} %convert_element_type.281), kind=kOutput, calls=%fused_computation.38 | convolution fusion | flops 2443442688 | bytes 21245952 | tf_op jit(solution)/shard_map/dot_general | solution.py:22
  132.0 4.5 convolution_convert_fusion.2
  137.0 1.9 collective-permute-done.5
  145.6 6.3 %fusion.10 = f32[6,64,1024]{2,1,0:T(8,128)S(1)} fusion(bf16[512,6,64]{0,2,1:T(8,128)(2,1)S(1)} %bitcast.184, f32[6,512,1024]{2,1,0:T(8,128)} %copy-done.2, f32[6,512]{1,0:T(8,128)S(1)} %log_add_fusion.1, pred[512,1024]{1,0:T(8,128)(4,1)S(1)} %get-tuple-element.106), kind=kOutput, calls=%fused_computation.34 | convolution fusion | flops 412090368 | bytes 15085568 | tf_op jit(solution)/shard_map/hqk,qhe->khe/dot_general | solution.py:95
  151.9 9.6 %multiply_reduce_fusion.2 = (f32[6,512]{1,0:T(8,128)S(1)}, f32[6,512,1024]{2,1,0:T(8,128)}) fusion(f32[6,512,1024]{2,1,0:T(8,128)} %copy-done.2, f32[6,512]{1,0:T(8,128)S(1)} %log_add_fusion.1, pred[512,1024]{1,0:T(8,128)(4,1)S(1)} %get-tuple-element.106, bf16[512,6,64]{0,2,1:T(8,128)(2,1)S(1)} %bitcast.185, bf16[1024,6,64]{0,2,1:T(8,128)(2,1)S(1)} %bitcast.194), kind=kOutput, calls=%fused_computation.6 | convolution fusion | flops 415233024 | bytes 26894336 | tf_op jit(solution)/shard_map/qhe,khe->hqk/dot_general | solution.py:84
  161.5 7.2 %multiply_reduce_fusion.3 = (f32[6,512]{1,0:T(8,128)S(1)}, f32[6,512,1024]{2,1,0:T(8,128)}) fusion(f32[6,512,1024]{2,1,0:T(8,128)S(1)} %get-tuple-element.116, f32[6,512]{1,0:T(8,128)S(1)} %log_add_fusion.2, pred[512,1024]{1,0:T(8,128)(4,1)S(1)} %get-tuple-element.99, bf16[512,6,64]{0,2,1:T(8,128)(2,1)S(1)} %bitcast.180, bf16[1024,6,64]{0,2,1:T(8,128)(2,1)S(1)} %bitcast.195), kind=kOutput, calls=%fused_computation.9 | convolution fusion | flops 415233024 | bytes 26894336 | tf_op jit(solution)/shard_map/qhe,khe->hqk/dot_general | solution.py:84
  168.7 6.8 %multiply_convert_fusion.3 = bf16[6,512,1024]{2,1,0:T(8,128)(2,1)S(1)} fusion(f32[6,512,1024]{2,1,0:T(8,128)} %get-tuple-element.121, f32[6,512,1024]{2,1,0:T(8,128)S(1)} %get-tuple-element.116, f32[6,512]{1,0:T(8,128)S(1)} %get-tuple-element.120, f32[6,512]{1,0:T(8,128)S(1)} %log_add_fusion.2, pred[512,1024]{1,0:T(8,128)(4,1)S(1)} %get-tuple-element.99), kind=kLoop, calls=%fused_computation.8 | loop fusion | flops 15728640 | bytes 32006144 | tf_op jit(solution)/shard_map/convert_element_type | solution.py:88
  175.5 2.1 convolution_convert_fusion.11
  178.1 10.0 %multiply_convert_fusion.2 = bf16[6,512,1024]{2,1,0:T(8,128)(2,1)S(1)} fusion(f32[6,512,1024]{2,1,0:T(8,128)} %get-tuple-element.119, f32[6,512,1024]{2,1,0:T(8,128)} %copy-done.2, f32[6,512]{1,0:T(8,128)S(1)} %get-tuple-element.118, f32[6,512]{1,0:T(8,128)S(1)} %log_add_fusion.1, pred[512,1024]{1,0:T(8,128)(4,1)S(1)} %get-tuple-element.106), kind=kLoop, calls=%fused_computation.5 | loop fusion | flops 15728640 | bytes 32006144 | tf_op jit(solution)/shard_map/convert_element_type | solution.py:88
  188.1 2.1 convolution_convert_fusion.10
  193.2 4.0 convert_reduce_fusion.4
  199.4 4.1 fusion.105
  203.6 3.1 multiply_reduce_fusion.6
  212.5 2.7 copy.60
  218.5 6.9 %fusion.8 = f32[6,64,1024]{2,1,0:T(8,128)S(1)} fusion(bf16[512,6,64]{0,2,1:T(8,128)(2,1)S(1)} %bitcast.186, f32[6,512,1024]{2,1,0:T(8,128)} %copy-done.4, f32[6,512]{1,0:T(8,128)S(1)} %copy-done.96, pred[512,1024]{1,0:T(8,128)(4,1)S(1)} %copy-done.16), kind=kOutput, calls=%fused_computation.33 | convolution fusion | flops 412090368 | bytes 15085568 | tf_op jit(solution)/shard_map/hqk,qhe->khe/dot_general | solution.py:95
  225.4 9.8 %multiply_reduce_fusion = (f32[6,512]{1,0:T(8,128)S(1)}, f32[6,512,1024]{2,1,0:T(8,128)}) fusion(f32[6,512,1024]{2,1,0:T(8,128)} %copy-done.4, f32[6,512]{1,0:T(8,128)S(1)} %copy-done.96, pred[512,1024]{1,0:T(8,128)(4,1)S(1)} %copy-done.16, bf16[512,6,64]{0,2,1:T(8,128)(2,1)S(1)} %bitcast.187, bf16[1024,6,64]{0,2,1:T(8,128)(2,1)S(1)} %bitcast.190), kind=kOutput, calls=%fused_computation.1 | convolution fusion | flops 415233024 | bytes 26894336 | tf_op jit(solution)/shard_map/qhe,khe->hqk/dot_general | solution.py:84
  235.2 7.4 %multiply_reduce_fusion.1 = (f32[6,512]{1,0:T(8,128)S(1)}, f32[6,512,1024]{2,1,0:T(8,128)}) fusion(f32[6,512,1024]{2,1,0:T(8,128)S(1)} %bitcast.151, f32[6,512]{1,0:T(8,128)S(1)} %log_add_fusion.3, pred[512,1024]{1,0:T(8,128)(4,1)S(1)} %copy-done.14, bf16[512,6,64]{0,2,1:T(8,128)(2,1)S(1)} %bitcast.182, bf16[1024,6,64]{0,2,1:T(8,128)(2,1)S(1)} %bitcast.191), kind=kOutput, calls=%fused_computation.4 | convolution fusion | flops 415233024 | bytes 26894336 | tf_op jit(solution)/shard_map/qhe,khe->hqk/dot_general | solution.py:84
  242.6 17.7 %multiply_convert_fusion = (bf16[6,512,1024]{2,1,0:T(8,128)(2,1)}, bf16[6,512,1024]{2,1,0:T(8,128)(2,1)}) fusion(f32[6,512,1024]{2,1,0:T(8,128)} %get-tuple-element.123, f32[6,512,1024]{2,1,0:T(8,128)} %copy-done.4, f32[6,512]{1,0:T(8,128)S(1)} %get-tuple-element.122, f32[6,512]{1,0:T(8,128)S(1)} %copy-done.96, pred[512,1024]{1,0:T(8,128)(4,1)S(1)} %copy-done.16, ...), kind=kLoop, calls=%fused_computation | loop fusion | flops 31457280 | bytes 64012288 | tf_op jit(solution)/shard_map/convert_element_type | solution.py:88
  260.4 5.7 convolution_convert_fusion.9
  266.1 2.4 fusion.103
  268.5 4.0 convert_reduce_fusion.7
  273.4 1.8 convolution_bitcast_fusion.2
  275.2 2.7 copy.57
  277.9 5.7 convolution_convert_fusion.8
  283.6 4.2 add_convert_fusion.7
  287.8 1.8 convolution_bitcast_fusion.3
  291.3 3.3 convolution_bitcast_fusion.4
  294.6 2.8 copy.55
  297.4 2.6 constant_dynamic-update-slice_fusion.4
  302.4 2.1 convolution_dynamic-update-slice_fusion.4
  304.5 2.3 convolution_dynamic-update-slice_fusion.3
  309.1 2.1 convolution_dynamic-update-slice_fusion.2
  311.9 4.3 convolution_dynamic-update-slice_fusion.1
  316.2 4.4 convolution_dynamic-update-slice_fusion
  322.9 2.2 add_convert_fusion.1
  332.1 3.0 convert_add_fusion
  335.9 46.4 %all-reduce = (f32[768]{0:T(1024)S(1)}, f32[768]{0:T(1024)S(1)}, f32[768]{0:T(1024)}, f32[768]{0:T(1024)S(1)}, f32[768]{0:T(1024)S(1)}, /*index=5*/f32[768]{0:T(...) all-reduce(f32[768]{0:T(1024)S(1)} %dynamic_update_slice.15, ...), channel_id=1, replica_groups=mesh['dp'=16,'tensor'=2] {'dp','tensor'}, use_global_device_ids=true, to_apply=%region_26.27 | all-reduce | flops 13056 | bytes 104448 | tf_op jit(solution)/shard_map/psum | solution.py:321
  385.6 3.9 add_add_fusion.4
  389.5 220.1 %reduce-scatter.2.cloned.1.call-done = f32[48,6144]{1,0:T(8,128)} async-done(((f32[768,6144]{1,0:T(8,128)}), f32[48,6144]{1,0:T(8,128)}) %reduce-scatter.2.cloned.1.call-update) | async-done | bytes 1179664 | tf_op jit(solution)/shard_map/reduce_scatter | solution.py:305
  609.5 1.9 slice_bitcast_fusion.1
  611.5 1.9 slice_bitcast_fusion
  (426 shorter events, 71.8 us)
Async XLA Ops:
  7.2 81.6 %copy-start = (bf16[768,1536]{1,0:T(8,128)(2,1)S(1)}, bf16[768,1536]{1,0:T(8,128)(2,1)}, u32[]{:S(2)}) copy-start(bf16[768,1536]{1,0:T(8,128)(2,1)} %param.52) | copy-start | bytes 7077892
  7.2 4.9 copy-start.89
  7.2 602.3 %reduce-scatter.2.cloned.1.call-start = ((), (), s32[]{:S(2)}) async-start(), calls=%async_computation.1 | async-start | bytes 20054016 | tf_op jit(solution)/shard_map/reduce_scatter | solution.py:305
  7.3 4.9 copy-start.93
  12.2 15.2 %copy-start.36 = (bf16[512,384]{0,1:T(8,128)(2,1)}, bf16[512,384]{0,1:T(8,128)(2,1)S(1)}, u32[]{:S(2)}) copy-start(bf16[512,384]{0,1:T(8,128)(2,1)S(1)} %get-tuple-element.98) | copy-start | bytes 1179652
  13.3 14.1 %copy-start.23 = (bf16[1024,384]{0,1:T(8,128)(2,1)}, bf16[1024,384]{0,1:T(8,128)(2,1)S(1)}, u32[]{:S(2)}) copy-start(bf16[1024,384]{0,1:T(8,128)(2,1)S(1)} %convolution_convert_fusion.7) | copy-start | bytes 2359300
  14.1 18.7 %copy-start.51 = (bf16[1024,384]{0,1:T(8,128)(2,1)}, bf16[1024,384]{0,1:T(8,128)(2,1)S(1)}, u32[]{:S(2)}) copy-start(bf16[1024,384]{0,1:T(8,128)(2,1)S(1)} %add_convert_fusion.10) | copy-start | bytes 2359300
  15.7 5.6 copy-start.13
  15.7 17.2 %copy-start.15 = (pred[512,1024]{1,0:T(8,128)(4,1)}, pred[512,1024]{1,0:T(8,128)(4,1)S(1)}, u32[]{:S(2)}) copy-start(pred[512,1024]{1,0:T(8,128)(4,1)S(1)} %get-tuple-element.105) | copy-start | bytes 1572868
  21.2 6.1 copy-start.105
  46.2 3.9 collective-permute-start
  46.7 37.6 %copy-start.97 = (f32[768]{0:T(1024)}, f32[768]{0:T(1024)S(1)}, u32[]{:S(2)}) copy-start(f32[768]{0:T(1024)S(1)} %convert_element_type.262) | copy-start | bytes 9220
  53.0 31.3 %copy-start.5 = (f32[512,768]{1,0:T(8,128)}, f32[512,768]{1,0:T(8,128)S(1)}, u32[]{:S(2)}) copy-start(f32[512,768]{1,0:T(8,128)S(1)} %get-tuple-element.71) | copy-start | bytes 4718596
  53.1 31.3 %copy-start.101 = (f32[512]{0:T(512)}, f32[512]{0:T(512)S(1)}, u32[]{:S(2)}) copy-start(f32[512]{0:T(512)S(1)} %broadcast_multiply_fusion.5) | copy-start | bytes 6148
  53.5 30.9 %copy-start.103 = (f32[512]{0:T(512)}, f32[512]{0:T(512)S(1)}, u32[]{:S(2)}) copy-start(f32[512]{0:T(512)S(1)} %fusion.60) | copy-start | bytes 6148
  53.8 3.2 collective-permute-start.1
  56.1 13.6 %copy-start.25 = (bf16[1024,384]{0,1:T(8,128)(2,1)}, bf16[1024,384]{0,1:T(8,128)(2,1)S(1)}, u32[]{:S(2)}) copy-start(bf16[1024,384]{0,1:T(8,128)(2,1)S(1)} %convolution_convert_fusion.6) | copy-start | bytes 2359300
  57.0 18.7 %copy-start.53 = (bf16[1024,384]{0,1:T(8,128)(2,1)}, bf16[1024,384]{0,1:T(8,128)(2,1)S(1)}, u32[]{:S(2)}) copy-start(bf16[1024,384]{0,1:T(8,128)(2,1)S(1)} %add_convert_fusion.9) | copy-start | bytes 2359300
  58.7 10.9 %copy-start.42 = (bf16[512,384]{0,1:T(8,128)(2,1)}, bf16[512,384]{0,1:T(8,128)(2,1)S(1)}, u32[]{:S(2)}) copy-start(bf16[512,384]{0,1:T(8,128)(2,1)S(1)} %get-tuple-element.95) | copy-start | bytes 1179652
  75.7 5.2 copy-start.142
  82.0 2.4 collective-permute-start.2
  85.9 2.4 collective-permute-start.3
  88.7 23.9 %copy-start.28 = (bf16[512,768]{1,0:T(8,128)(2,1)}, bf16[512,768]{1,0:T(8,128)(2,1)S(1)}, u32[]{:S(2)}) copy-start(bf16[512,768]{1,0:T(8,128)(2,1)S(1)} %get-tuple-element.77) | copy-start | bytes 2359300
  88.7 23.9 %copy-start.30 = (bf16[512,768]{1,0:T(8,128)(2,1)}, bf16[512,768]{1,0:T(8,128)(2,1)S(1)}, u32[]{:S(2)}) copy-start(bf16[512,768]{1,0:T(8,128)(2,1)S(1)} %get-tuple-element.78) | copy-start | bytes 2359300
  88.8 17.7 %copy-start.138 = (bf16[1536,768]{1,0:T(8,128)(2,1)S(1)}, bf16[1536,768]{1,0:T(8,128)(2,1)}, u32[]{:S(2)}) copy-start(bf16[1536,768]{1,0:T(8,128)(2,1)} %param.54) | copy-start | bytes 7077892
  109.1 3.5 collective-permute-start.4
  120.8 18.1 %copy-start.11 = (f32[1024,768]{1,0:T(8,128)}, f32[1024,768]{1,0:T(8,128)S(1)}, u32[]{:S(2)}) copy-start(f32[1024,768]{1,0:T(8,128)S(1)} %get-tuple-element.53) | copy-start | bytes 9437188
  136.6 2.4 collective-permute-start.5
  142.0 2.3 collective-permute-start.6
  145.6 6.3 %copy-start.54 = (bf16[1024,384]{0,1:T(8,128)(2,1)S(1)}, bf16[1024,384]{0,1:T(8,128)(2,1)}, u32[]{:S(2)}) copy-start(bf16[1024,384]{0,1:T(8,128)(2,1)} %copy-done.53) | copy-start | bytes 2359300
  168.7 6.8 %copy-start.26 = (bf16[1024,384]{0,1:T(8,128)(2,1)S(1)}, bf16[1024,384]{0,1:T(8,128)(2,1)}, u32[]{:S(2)}) copy-start(bf16[1024,384]{0,1:T(8,128)(2,1)} %copy-done.25) | copy-start | bytes 2359300
  178.1 12.6 %copy-start.64 = (bf16[6,64,512]{2,1,0:T(8,128)(2,1)}, bf16[6,64,512]{2,1,0:T(8,128)(2,1)S(1)}, u32[]{:S(2)}) copy-start(bf16[6,64,512]{2,1,0:T(8,128)(2,1)S(1)} %convolution_convert_fusion.11) | copy-start | bytes 1179652
  190.7 6.5 %copy-start.67 = (bf16[6,64,512]{2,1,0:T(8,128)(2,1)}, bf16[6,64,512]{2,1,0:T(8,128)(2,1)S(1)}, u32[]{:S(2)}) copy-start(bf16[6,64,512]{2,1,0:T(8,128)(2,1)S(1)} %convolution_convert_fusion.10) | copy-start | bytes 1179652
  191.7 5.5 copy-start.32
  192.8 5.3 copy-start.140
  192.8 10.7 %collective-permute-start.7 = (bf16[512,768]{1,0:T(8,128)(2,1)}, bf16[512,768]{1,0:T(8,128)(2,1)}, u32[]{:S(2)}, u32[]{:S(2)}) collective-permute-start(bf16[512,768]{1,0:T(8,128)(2,1)} %broadcast_select_fusion.4), channel_id=1, source_target_pairs={{0,1},{1,0},{2,3},{3,2},{4,5},{5,4},{6,7},{7,6},{8,9},{9,8},{10,11... | collective-permute-start | bytes 2359304 | tf_op jit(solution)/shard_map/ppermute | solution.py:151
  199.4 10.1 %slice-start.3 = ((s8[6291456]{0:T(1024)(128)(4,1)}), s8[4194304]{0:T(1024)(128)(4,1)S(1)}, s32[]{:S(2)}) async-start(s8[6291456]{0:T(1024)(128)(4,1)} %bitcast.152), calls=%async_computation.5 | async-start | bytes 8388608
  203.6 5.9 slice-start.4
  209.3 5.9 collective-permute-start.8
  218.5 6.9 %copy-start.52 = (bf16[1024,384]{0,1:T(8,128)(2,1)S(1)}, bf16[1024,384]{0,1:T(8,128)(2,1)}, u32[]{:S(2)}) copy-start(bf16[1024,384]{0,1:T(8,128)(2,1)} %copy-done.51) | copy-start | bytes 2359300
  218.5 16.7 %slice-start = ((s8[12582912]{0:T(1024)(128)(4,1)}), s8[4194304]{0:T(1024)(128)(4,1)S(1)}, s32[]{:S(2)}) async-start(s8[12582912]{0:T(1024)(128)(4,1)} %bitcast.150), calls=%async_computation.2 | async-start | bytes 8388608
  218.5 16.7 %slice-start.1 = ((s8[12582912]{0:T(1024)(128)(4,1)}), s8[4194304]{0:T(1024)(128)(4,1)S(1)}, s32[]{:S(2)}) async-start(s8[12582912]{0:T(1024)(128)(4,1)} %bitcast.150), calls=%async_computation.3 | async-start | bytes 8388608
  225.4 9.8 %slice-start.2 = ((s8[12582912]{0:T(1024)(128)(4,1)}), s8[4194304]{0:T(1024)(128)(4,1)S(1)}, s32[]{:S(2)}) async-start(s8[12582912]{0:T(1024)(128)(4,1)} %bitcast.150), calls=%async_computation.4 | async-start | bytes 8388608
  225.4 9.8 %copy-start.14 = (pred[512,1024]{1,0:T(8,128)(4,1)S(1)}, pred[512,1024]{1,0:T(8,128)(4,1)}, u32[]{:S(2)}) copy-start(pred[512,1024]{1,0:T(8,128)(4,1)} %copy-done.13) | copy-start | bytes 1572868
  242.6 17.8 %copy-start.24 = (bf16[1024,384]{0,1:T(8,128)(2,1)S(1)}, bf16[1024,384]{0,1:T(8,128)(2,1)}, u32[]{:S(2)}) copy-start(bf16[1024,384]{0,1:T(8,128)(2,1)} %copy-done.23) | copy-start | bytes 2359300
  260.4 5.7 copy-start.9
  260.4 5.7 copy-start.41
  268.5 4.9 copy-start.94
  277.9 5.7 copy-start.27
  277.9 5.7 copy-start.37
  294.6 6.6 %copy-start.35 = (f32[768,384]{1,0:T(8,128)S(1)}, f32[768,384]{1,0:T(8,128)}, u32[]{:S(2)}) copy-start(f32[768,384]{1,0:T(8,128)} %copy.57) | copy-start | bytes 3538948
  297.4 4.9 copy-start.63
  297.4 4.9 copy-start.81
  297.4 4.9 copy-start.83
  326.1 6.0 collective-permute-start.10
  330.0 5.2 copy-start.18
  330.0 5.2 copy-start.122
  331.1 4.8 copy-start.116
  331.1 4.8 copy-start.117
  331.1 4.8 copy-start.118
  331.1 4.8 copy-start.119
  331.1 54.5 %copy-start.110 = (f32[512]{0:T(512)S(1)}, f32[512]{0:T(512)}, u32[]{:S(2)}) copy-start(f32[512]{0:T(512)} %copy-done.109) | copy-start | bytes 6148
  331.1 54.5 %collective-permute-start.9 = (bf16[512,768]{1,0:T(8,128)(2,1)}, bf16[512,768]{1,0:T(8,128)(2,1)}, u32[]{:S(2)}, u32[]{:S(2)}) collective-permute-start(bf16[512,768]{1,0:T(8,128)(2,1)} %broadcast_select_fusion.1), channel_id=1, source_target_pairs={{0,1},{1,0},{2,3},{3,2},{4,5},{5,4},{6,7},{7,6},{8,9},{9,8},{10,11... | collective-permute-start | bytes 2359304 | tf_op jit(solution)/shard_map/ppermute | solution.py:151
  384.9 228.5 %copy-start.1 = (bf16[768,1536]{1,0:T(8,128)(2,1)S(1)}, bf16[768,1536]{1,0:T(8,128)(2,1)}, u32[]{:S(2)}) copy-start(bf16[768,1536]{1,0:T(8,128)(2,1)} %param.52) | copy-start | bytes 7077892
  (99 other events, 248.9 us)
Sparse Core Ops, SparseCore 0:
  320.7 288.7 reduce-scatter.1

commit v3 on v2

--- a/solution.py
+++ b/solution.py
@@ -244,8 +244,8 @@
     )
     grad_second_in, grad_second_gain, grad_second_shift = second_back(grad_second)
     grad_cross_rows = grad_second_in.astype(jnp.bfloat16)
-    grad_cross_output_bias = column_sums(grad_cross_rows)
     grad_cross = gather_rows(grad_cross_rows)
+    grad_cross_output_bias = column_sums(grad_cross)
     grad_cross_context = heads_of(project(grad_cross, cross_output.T).astype(jnp.bfloat16))
     cross_grad_q, cross_grad_k, cross_grad_v = attend_backward(
         cross_queries, cross_keys, cross_values, grad_cross_context, cross_totals, segment, False
@@ -264,8 +264,8 @@
     )
     grad_first_in, grad_first_gain, grad_first_shift = first_back(grad_first)
     grad_self_rows = grad_first_in.astype(jnp.bfloat16)
-    grad_self_output_bias = column_sums(grad_self_rows)
     grad_self = gather_rows(grad_self_rows)
+    grad_self_output_bias = column_sums(grad_self)
     grad_self_context = heads_of(project(grad_self, self_output.T).astype(jnp.bfloat16))
     self_grad_q, self_grad_k, self_grad_v = attend_backward(
         self_queries, self_keys, self_values, grad_self_context, self_totals, segment, True
@@ -289,11 +289,8 @@
     grad_self_output_t = project(grad_self.T, self_context)
     grad_cross_output_t = project(grad_cross.T, cross_context)
     grad_outer_weight_t = project(grad_outer.T, hidden)
-    gathered = [
-        grad_self_query,
-        grad_self_key,
-        grad_self_value,
-        grad_self_output_t,
+    dp_size = lax.axis_size("dp")
+    early = [
         grad_cross_query,
         grad_cross_key,
         grad_cross_value,
@@ -301,58 +298,100 @@
         grad_inner_weight,
         grad_outer_weight_t,
     ]
-    widths = [piece.shape[1] for piece in gathered]
-    summed = lax.psum_scatter(
-        jnp.concatenate(gathered, 1), "dp", scatter_dimension=0, tiled=True
-    )
-    everything = []
+    early_widths = [piece.shape[1] for piece in early]
+    early_sum = lax.psum_scatter(
+        jnp.concatenate(early, 1).astype(jnp.bfloat16), "dp", scatter_dimension=0, tiled=True
+    ).astype(jnp.float32)
+    early_parts = []
     offset = 0
-    for position, width in enumerate(widths):
-        piece = summed[:, offset : offset + width]
+    for position, width in enumerate(early_widths):
+        piece = early_sum[:, offset : offset + width]
         offset += width
-        if position in (3, 7, 9):
+        if position in (3, 5):
             piece = piece.T
-        everything.append(piece)
-    self_sums = everything[0:4]
-    cross_sums = everything[4:8]
-    ffn_sums = everything[8:10]
-    head_columns = grad_self_query_bias.shape[0]
-    unit_columns = grad_inner_bias.shape[0]
-    smalls = lax.psum(
-        (
-            spread_out(grad_self_query_bias),
-            spread_out(grad_self_value_bias),
+        early_parts.append(piece)
+    cross_sums = early_parts[0:4]
+    ffn_sums = early_parts[4:6]
+    late = jnp.concatenate(
+        [grad_self_query, grad_self_key, grad_self_value, grad_self_output_t], 1
+    )
+    late_rows = late.shape[0] // dp_size
+    late_width = late_rows * late.shape[1]
+    norm_pairs = sum_pair(
+        jnp.concatenate([grad_first_gain, grad_first_shift, grad_second_gain, grad_second_shift])
+    )
+    vector = jnp.concatenate(
+        [
+            grad_self_query_bias,
+            grad_self_value_bias,
             grad_self_output_bias,
-            spread_out(grad_cross_query_bias),
-            spread_out(grad_cross_value_bias),
+            grad_cross_query_bias,
+            grad_cross_value_bias,
             grad_cross_output_bias,
-            grad_first_gain,
-            grad_first_shift,
-            grad_second_gain,
-            grad_second_shift,
-            grad_third_gain * 0.5,
-            grad_third_shift * 0.5,
-            spread_out(grad_inner_bias),
-            grad_outer_bias * 0.5,
-        ),
-        ("dp", "tensor"),
-    )
+            norm_pairs,
+            grad_third_gain,
+            grad_third_shift,
+            grad_inner_bias,
+            grad_outer_bias,
+        ]
+    )
+    packed = jnp.concatenate(
+        [
+            late.reshape(dp_size, late_width),
+            jnp.broadcast_to(vector[None], (dp_size, vector.shape[0])),
+        ],
+        1,
+    )
+    received = lax.all_to_all(packed, "dp", 0, 0, tiled=True)
+    total = jnp.sum(received, 0)
+    late_sum = total[:late_width].reshape(late_rows, late.shape[1])
+    self_sums = []
+    offset = 0
+    for position in range(4):
+        width = (grad_self_query, grad_self_key, grad_self_value, grad_self_output_t)[
+            position
+        ].shape[1]
+        piece = late_sum[:, offset : offset + width]
+        offset += width
+        if position == 3:
+            piece = piece.T
+        self_sums.append(piece)
+    smalls = []
+    offset = late_width
+    for piece in (
+        grad_self_query_bias,
+        grad_self_value_bias,
+        grad_self_output_bias,
+        grad_cross_query_bias,
+        grad_cross_value_bias,
+        grad_cross_output_bias,
+        grad_first_gain,
+        grad_first_shift,
+        grad_second_gain,
+        grad_second_shift,
+        grad_third_gain,
+        grad_third_shift,
+        grad_inner_bias,
+        grad_outer_bias,
+    ):
+        smalls.append(total[offset : offset + piece.shape[0]])
+        offset += piece.shape[0]
     return (
         output,
         grad_tokens,
         memory_part,
         self_sums[0],
-        own_share(smalls[0], head_columns),
+        smalls[0],
         self_sums[1],
         self_sums[2],
-        own_share(smalls[1], head_columns),
+        smalls[1],
         self_sums[3],
         smalls[2],
         cross_sums[0],
-        own_share(smalls[3], head_columns),
+        smalls[3],
         cross_sums[1],
         cross_sums[2],
-        own_share(smalls[4], head_columns),
+        smalls[4],
         cross_sums[3],
         smalls[5],
         smalls[6],
@@ -362,7 +401,7 @@
         smalls[10],
         smalls[11],
         ffn_sums[0],
-        own_share(smalls[12], unit_columns),
+        smalls[12],
         ffn_sums[1],
         smalls[13],
     )

time: 630 us -> 532 us (0.84)
  the two profiles are of different devices: /device:TPU:0 before, /device:TPU:12 now
where the time goes in v3:
time: 532 us; the launch traced here: 523 us
  matrix products  192 us (36%)
  waiting for transfers between devices  119 us (22%)
  other arithmetic  109 us (20%)
  local copies, waits for them, and re-layouts  75 us (14%)
  between operations  16.7 us (3%)
  starting transfers between devices  11.4 us (2%)
    all_to_all x1, waiting for transfers between devices, on_device(): received = lax.all_to_all(packed, 'dp', 0, 0, tiled=True)  113 us
    dot_general x30, matrix products, project(): return jnp.dot(data, weight, preferred_element_type=jnp.float32)  75.4 us
    convert_element_type x3, other arithmetic, attend_backward(): grad_scores = (probs * (grad_probs - row_inner)).astype(jnp.bfloat16)  36.7 us
    unnamed x334, local copies, waits for them, and re-layouts  36.6 us
    dot_general x4, matrix products, attend_backward(): jnp.einsum('qhe,khe->hqk', grad_piece, values, preferred_element_type=jnp...  35.2 us
    dot_general x4, matrix products, attend_backward(): jnp.einsum('hqk,qhe->khe', probs.astype(jnp.bfloat16), grad_piece, prefer...  22.6 us
    dot_general x4, matrix products, attend_backward(): jnp.einsum('hqk,qhe->khe', grad_scores, piece, preferred_element_type=jnp...  18.2 us
    dot_general x4, matrix products, attend_forward(): jnp.einsum('hqk,khe->qhe', weights, values, preferred_element_type=jnp.fl...  17.9 us
  transfers between devices with their start and end apart: 14, of which 5 were waited for; matrix products, arithmetic and copies ran while one was open for 31% of the time, Pallas kernels for 0%

profile of v3, /device:TPU:12, one launch (start us, length us, event | category | flops | bytes accessed | tf_op | source)
XLA Modules:
  0.0 522.8 jit_solution(8811667212092640426)
XLA Ops:
  9.7 2.4 multiply_convert_fusion.6
  15.7 2.1 select_reduce_fusion.3
  17.9 3.4 fusion
  22.6 4.7 fusion.57
  27.4 2.1 select_reduce_fusion.2
  29.5 3.4 fusion.1
  34.1 4.9 fusion.58
  41.1 2.1 fusion.110
  46.5 2.1 constant_dynamic-slice_fusion
  48.5 2.3 copy.121
  50.8 2.9 fusion.101
  59.4 2.1 select_reduce_fusion
  61.5 3.4 fusion.3
  66.0 4.1 fusion.60
  70.2 2.1 select_reduce_fusion.1
  72.3 3.8 fusion.2
  76.8 4.1 fusion.59
  88.9 18.2 %multiply_convert_fusion.4 = (bf16[1024,1536]{1,0:T(8,128)(2,1)S(1)}, f32[1024,1536]{1,0:T(8,128)}, f32[1024,1536]{1,0:T(8,128)}) fusion(f32[1536]{0:T(1024)S(1)} %convert_element_type.285, bf16[768,1536]{1,0:T(8,128)(2,1)S(1)} %copy-done, bf16[512,768]{0,1:T(8,128)(2,1)S(1)} %get-tuple-element.141, bf16[512,768]{0,1:T(8,128)(2,1)S(1)} %get-tuple-element.140), kind=kOutput, calls=%fused_computation.44 | convolution fusion | flops 2522873856 | bytes 19666944 | tf_op jit(solution)/shard_map/dot_general | solution.py:22
  107.1 3.8 convolution_convert_fusion.5
  111.3 2.7 copy.95
  114.6 3.1 fusion.98
  119.4 2.2 fusion.43
  121.5 3.2 convert_reduce_fusion.2
  124.8 8.6 %convert_reduce_fusion = (f32[1536]{0:T(1024)}, bf16[1024,1536]{1,0:T(8,128)(2,1)S(1)}) fusion(f32[1024,1536]{1,0:T(8,128)S(1)} %bitcast.217, bf16[1536,768]{1,0:T(8,128)(2,1)S(1)} %copy-done.135, f32[1024,768]{0,1:T(8,128)S(1)} %get-tuple-element.120, f32[1024,1536]{1,0:T(8,128)} %get-tuple-element.190, f32[1536]{0:T(1024)S(1)} %convert_element_type.285), kind=kOutput, calls=%fused_computation.38 | convolution fusion | flops 2443442688 | bytes 21245952 | tf_op jit(solution)/shard_map/dot_general | solution.py:22
  133.4 2.6 convolution_convert_fusion.4
  148.9 11.5 %multiply_reduce_fusion.3 = (f32[6,512]{1,0:T(8,128)S(1)}, f32[6,512,1024]{2,1,0:T(8,128)}) fusion(f32[6,512,1024]{2,1,0:T(8,128)} %copy-done.2, f32[6,512]{1,0:T(8,128)S(1)} %log_add_fusion.2, pred[512,1024]{1,0:T(8,128)(4,1)S(1)} %get-tuple-element.172, bf16[512,6,64]{0,2,1:T(8,128)(2,1)S(1)} %bitcast.188, bf16[1024,6,64]{0,2,1:T(8,128)(2,1)S(1)} %bitcast.202), kind=kOutput, calls=%fused_computation.9 | convolution fusion | flops 415233024 | bytes 26894336 | tf_op jit(solution)/shard_map/qhe,khe->hqk/dot_general | solution.py:84
  161.1 10.4 %multiply_convert_fusion.3 = bf16[6,512,1024]{2,1,0:T(8,128)(2,1)} fusion(f32[6,512,1024]{2,1,0:T(8,128)} %get-tuple-element.194, f32[6,512,1024]{2,1,0:T(8,128)S(1)} %bitcast.153, f32[6,512]{1,0:T(8,128)S(1)} %get-tuple-element.193, f32[6,512]{1,0:T(8,128)S(1)} %log_add_fusion.2, pred[512,1024]{1,0:T(8,128)(4,1)S(1)} %get-tuple-element.172), kind=kLoop, calls=%fused_computation.8 | loop fusion | flops 15728640 | bytes 32006144 | tf_op jit(solution)/shard_map/convert_element_type | solution.py:88
  171.5 5.0 convolution_convert_fusion.17
  176.5 4.2 fusion.112
  180.7 4.0 fusion.10
  184.7 6.7 %multiply_reduce_fusion.2 = (f32[6,512]{1,0:T(8,128)S(1)}, f32[6,512,1024]{2,1,0:T(8,128)}) fusion(f32[6,512,1024]{2,1,0:T(8,128)S(1)} %bitcast.155, f32[6,512]{1,0:T(8,128)S(1)} %log_add_fusion.1, pred[512,1024]{1,0:T(8,128)(4,1)S(1)} %get-tuple-element.179, bf16[512,6,64]{0,2,1:T(8,128)(2,1)S(1)} %bitcast.193, bf16[1024,6,64]{0,2,1:T(8,128)(2,1)S(1)} %bitcast.203), kind=kOutput, calls=%fused_computation.6 | convolution fusion | flops 415233024 | bytes 26894336 | tf_op jit(solution)/shard_map/qhe,khe->hqk/dot_general | solution.py:84
  191.5 7.1 %multiply_convert_fusion.2 = bf16[6,512,1024]{2,1,0:T(8,128)(2,1)S(1)} fusion(f32[6,512,1024]{2,1,0:T(8,128)} %get-tuple-element.192, f32[6,512,1024]{2,1,0:T(8,128)S(1)} %bitcast.155, f32[6,512]{1,0:T(8,128)S(1)} %get-tuple-element.191, f32[6,512]{1,0:T(8,128)S(1)} %log_add_fusion.1, pred[512,1024]{1,0:T(8,128)(4,1)S(1)} %get-tuple-element.179), kind=kLoop, calls=%fused_computation.5 | loop fusion | flops 15728640 | bytes 32006144 | tf_op jit(solution)/shard_map/convert_element_type | solution.py:88
  202.9 2.2 convolution_convert_fusion.2
  206.1 7.8 %convert_reduce_fusion.5 = (f32[6,64]{1,0:T(8,128)S(1)}, bf16[6,64,1024]{2,1,0:T(8,128)(2,1)}) fusion(f32[6,64,1024]{2,1,0:T(8,128)} %fusion.10, bf16[512,6,64]{0,2,1:T(8,128)(2,1)S(1)} %bitcast.189, f32[6,512,1024]{2,1,0:T(8,128)} %copy-done.2, f32[6,512]{1,0:T(8,128)S(1)} %log_add_fusion.2, pred[512,1024]{1,0:T(8,128)(4,1)S(1)} %get-tuple-element.172), kind=kOutput, calls=%fused_computation.108 | convolution fusion | flops 413662848 | bytes 15873536 | tf_op jit(solution)/shard_map/hqk,qhe->khe/dot_general | solution.py:95
  214.5 2.5 fusion.52
  218.1 4.0 add_convert_fusion.5
  222.1 2.1 copy.105
  224.2 2.3 fusion.51
  227.9 2.1 constant_dynamic-update-slice_fusion.4
  232.9 3.9 fusion.41
  242.2 4.0 fusion.40
  257.9 6.4 %fusion.8 = f32[6,64,1024]{2,1,0:T(8,128)S(1)} fusion(bf16[512,6,64]{0,2,1:T(8,128)(2,1)S(1)} %bitcast.194, f32[6,512,1024]{2,1,0:T(8,128)} %copy-done.5, f32[6,512]{1,0:T(8,128)S(1)} %copy-done.89, pred[512,1024]{1,0:T(8,128)(4,1)S(1)} %copy-done.20), kind=kOutput, calls=%fused_computation.33 | convolution fusion | flops 412090368 | bytes 15085568 | tf_op jit(solution)/shard_map/hqk,qhe->khe/dot_general | solution.py:95
  264.4 9.8 %multiply_reduce_fusion = (f32[6,512]{1,0:T(8,128)S(1)}, f32[6,512,1024]{2,1,0:T(8,128)}) fusion(f32[6,512,1024]{2,1,0:T(8,128)} %copy-done.5, f32[6,512]{1,0:T(8,128)S(1)} %copy-done.89, pred[512,1024]{1,0:T(8,128)(4,1)S(1)} %copy-done.20, bf16[512,6,64]{0,2,1:T(8,128)(2,1)S(1)} %bitcast.195, bf16[1024,6,64]{0,2,1:T(8,128)(2,1)S(1)} %bitcast.198), kind=kOutput, calls=%fused_computation.1 | convolution fusion | flops 415233024 | bytes 26894336 | tf_op jit(solution)/shard_map/qhe,khe->hqk/dot_general | solution.py:84
  274.2 7.2 %multiply_reduce_fusion.1 = (f32[6,512]{1,0:T(8,128)S(1)}, f32[6,512,1024]{2,1,0:T(8,128)}) fusion(f32[6,512,1024]{2,1,0:T(8,128)S(1)} %bitcast.157, f32[6,512]{1,0:T(8,128)S(1)} %log_add_fusion.3, pred[512,1024]{1,0:T(8,128)(4,1)S(1)} %copy-done.18, bf16[512,6,64]{0,2,1:T(8,128)(2,1)S(1)} %bitcast.190, bf16[1024,6,64]{0,2,1:T(8,128)(2,1)S(1)} %bitcast.199), kind=kOutput, calls=%fused_computation.4 | convolution fusion | flops 415233024 | bytes 26894336 | tf_op jit(solution)/shard_map/qhe,khe->hqk/dot_general | solution.py:84
  281.4 19.2 %multiply_convert_fusion = (bf16[6,512,1024]{2,1,0:T(8,128)(2,1)}, bf16[6,512,1024]{2,1,0:T(8,128)(2,1)}) fusion(f32[6,512,1024]{2,1,0:T(8,128)} %get-tuple-element.196, f32[6,512,1024]{2,1,0:T(8,128)} %copy-done.5, f32[6,512]{1,0:T(8,128)S(1)} %get-tuple-element.195, f32[6,512]{1,0:T(8,128)S(1)} %copy-done.89, pred[512,1024]{1,0:T(8,128)(4,1)S(1)} %copy-done.20, ...), kind=kLoop, calls=%fused_computation | loop fusion | flops 31457280 | bytes 64012288 | tf_op jit(solution)/shard_map/convert_element_type | solution.py:88
  300.6 5.1 convolution_convert_fusion.15
  305.7 5.4 %fusion.111 = f32[6,64,1024]{2,1,0:T(8,128)} fusion(bf16[512,6,64]{0,2,1:T(8,128)(2,1)S(1)} %bitcast.175, bf16[6,512,1024]{2,1,0:T(8,128)(2,1)} %get-tuple-element.206), kind=kOutput, calls=%fused_computation.265 | convolution fusion | flops 402653184 | bytes 8257536 | tf_op jit(solution)/shard_map/hqk,qhe->khe/dot_general | solution.py:92
  315.3 4.4 convert_reduce_fusion.7
  319.8 2.5 convolution_bitcast_fusion
  322.3 4.7 add_convert_fusion.7
  329.0 2.5 pad_maximum_fusion
  331.5 6.1 %copy.103 = f32[768,1536]{1,0:T(8,128)} copy(f32[768,1536]{0,1:T(8,128)} %pad_maximum_fusion) | data formatting | bytes 9437184 | tf_op jit(solution)/shard_map/concatenate | solution.py:315
  337.7 4.4 reshape.404
  343.0 2.8 maximum_bitcast_fusion
  345.8 12.2 %copy.104 = f32[16,1,83712]{2,1,0:T(1,128)} copy(f32[16,1,83712]{2,0,1:T(8,128)S(1)} %maximum_bitcast_fusion) | data formatting | bytes 10715136 | tf_op jit(solution)/shard_map/all_to_all | solution.py:345
  358.0 7.4 %all-to-all-start = ((f32[16,1,83712]{2,1,0:T(1,128)}), f32[16,1,83712]{2,1,0:T(1,128)}, u32[]{:S(2)}, u32[]{:S(2)}) async-start(f32[16,1,83712]{2,1,0:T(1,128)} %copy.104), calls=%async_computation | async-start | bytes 10715136 | tf_op jit(solution)/shard_map/all_to_all | solution.py:345
  365.4 2.2 fusion.114
  374.2 2.6 copy.109
  376.8 3.1 convert_add_fusion
  379.9 3.0 copy.111
  382.9 3.3 add_add_fusion.4
  386.2 3.0 copy.110
  389.3 112.7 %all-to-all-done = f32[16,1,83712]{2,1,0:T(1,128)} async-done(((f32[16,1,83712]{2,1,0:T(1,128)}), f32[16,1,83712]{2,1,0:T(1,128)}, u32[]{:S(2)}, u32[]{:S(2)}) %all-to-all-start) | async-done | bytes 5357600 | tf_op jit(solution)/shard_map/all_to_all | solution.py:345
  501.9 6.0 %reduce_sum.403 = f32[83712]{0:T(1024)S(1)} reduce(f32[16,1,83712]{2,1,0:T(1,128)} %all-to-all-done, f32[]{:T(128)} %constant.14.clone.1), dimensions={0,1}, to_apply=%region_38.39 | reduce | flops 1255680 | bytes 5692420 | tf_op jit(solution)/shard_map/reduce_sum | solution.py:346
  (463 shorter events, 94.2 us)
Async XLA Ops:
  7.2 81.7 %copy-start = (bf16[768,1536]{1,0:T(8,128)(2,1)S(1)}, bf16[768,1536]{1,0:T(8,128)(2,1)}, u32[]{:S(2)}) copy-start(bf16[768,1536]{1,0:T(8,128)(2,1)} %param.52) | copy-start | bytes 7077892
  7.2 503.3 %reduce-scatter.2.cloned.1.call-start = ((), (), s32[]{:S(2)}) async-start(), calls=%async_computation.2 | async-start | bytes 7520256 | tf_op jit(solution)/shard_map/reduce_scatter | solution.py:302
  12.2 15.2 %copy-start.33 = (bf16[512,384]{0,1:T(8,128)(2,1)}, bf16[512,384]{0,1:T(8,128)(2,1)S(1)}, u32[]{:S(2)}) copy-start(bf16[512,384]{0,1:T(8,128)(2,1)S(1)} %get-tuple-element.151) | copy-start | bytes 1179652
  13.3 14.1 %copy-start.23 = (bf16[1024,384]{0,1:T(8,128)(2,1)}, bf16[1024,384]{0,1:T(8,128)(2,1)S(1)}, u32[]{:S(2)}) copy-start(bf16[1024,384]{0,1:T(8,128)(2,1)S(1)} %convolution_convert_fusion.9) | copy-start | bytes 2359300
  14.1 18.7 %copy-start.49 = (bf16[1024,384]{0,1:T(8,128)(2,1)}, bf16[1024,384]{0,1:T(8,128)(2,1)S(1)}, u32[]{:S(2)}) copy-start(bf16[1024,384]{0,1:T(8,128)(2,1)S(1)} %add_convert_fusion.10) | copy-start | bytes 2359300
  15.7 5.6 %copy-start.17 = (pred[512,1024]{1,0:T(8,128)(4,1)}, pred[512,1024]{1,0:T(8,128)(4,1)S(1)}, u32[]{:S(2)}) copy-start(pred[512,1024]{1,0:T(8,128)(4,1)S(1)} %get-tuple-element.173) | copy-start | bytes 1572868
  15.7 17.2 %copy-start.19 = (pred[512,1024]{1,0:T(8,128)(4,1)}, pred[512,1024]{1,0:T(8,128)(4,1)S(1)}, u32[]{:S(2)}) copy-start(pred[512,1024]{1,0:T(8,128)(4,1)S(1)} %get-tuple-element.178) | copy-start | bytes 1572868
  21.2 6.1 %copy-start.98 = (f32[6,512]{1,0:T(8,128)}, f32[6,512]{1,0:T(8,128)S(1)}, u32[]{:S(2)}) copy-start(f32[6,512]{1,0:T(8,128)S(1)} %fusion) | copy-start | bytes 36868
  46.4 4.4 collective-permute-start
  46.4 38.3 %copy-start.90 = (f32[768]{0:T(1024)}, f32[768]{0:T(1024)S(1)}, u32[]{:S(2)}) copy-start(f32[768]{0:T(1024)S(1)} %convert_element_type.266) | copy-start | bytes 9220
  53.8 31.0 %copy-start.6 = (f32[512,768]{0,1:T(8,128)}, f32[512,768]{0,1:T(8,128)S(1)}, u32[]{:S(2)}) copy-start(f32[512,768]{0,1:T(8,128)S(1)} %get-tuple-element.134) | copy-start | bytes 4718596
  53.8 30.9 %copy-start.94 = (f32[512]{0:T(512)}, f32[512]{0:T(512)S(1)}, u32[]{:S(2)}) copy-start(f32[512]{0:T(512)S(1)} %broadcast_multiply_fusion.2) | copy-start | bytes 6148
  54.1 30.6 %copy-start.96 = (f32[512]{0:T(512)}, f32[512]{0:T(512)S(1)}, u32[]{:S(2)}) copy-start(f32[512]{0:T(512)S(1)} %fusion.66) | copy-start | bytes 6148
  54.4 3.3 collective-permute-start.1
  56.8 13.4 %copy-start.25 = (bf16[1024,384]{0,1:T(8,128)(2,1)}, bf16[1024,384]{0,1:T(8,128)(2,1)S(1)}, u32[]{:S(2)}) copy-start(bf16[1024,384]{0,1:T(8,128)(2,1)S(1)} %convolution_convert_fusion.8) | copy-start | bytes 2359300
  57.7 18.4 %copy-start.51 = (bf16[1024,384]{0,1:T(8,128)(2,1)}, bf16[1024,384]{0,1:T(8,128)(2,1)S(1)}, u32[]{:S(2)}) copy-start(bf16[1024,384]{0,1:T(8,128)(2,1)S(1)} %add_convert_fusion.9) | copy-start | bytes 2359300
  59.3 10.8 %copy-start.39 = (bf16[512,384]{0,1:T(8,128)(2,1)}, bf16[512,384]{0,1:T(8,128)(2,1)S(1)}, u32[]{:S(2)}) copy-start(bf16[512,384]{0,1:T(8,128)(2,1)S(1)} %get-tuple-element.148) | copy-start | bytes 1179652
  64.9 5.3 %copy-start.100 = (f32[6,512]{1,0:T(8,128)}, f32[6,512]{1,0:T(8,128)S(1)}, u32[]{:S(2)}) copy-start(f32[6,512]{1,0:T(8,128)S(1)} %fusion.3) | copy-start | bytes 36868
  82.3 2.5 collective-permute-start.2
  86.0 2.4 collective-permute-start.3
  88.8 18.2 %copy-start.55 = (bf16[512,768]{0,1:T(8,128)(2,1)}, bf16[512,768]{0,1:T(8,128)(2,1)S(1)}, u32[]{:S(2)}) copy-start(bf16[512,768]{0,1:T(8,128)(2,1)S(1)} %get-tuple-element.140) | copy-start | bytes 2359300
  88.8 18.2 %copy-start.57 = (bf16[512,768]{0,1:T(8,128)(2,1)}, bf16[512,768]{0,1:T(8,128)(2,1)S(1)}, u32[]{:S(2)}) copy-start(bf16[512,768]{0,1:T(8,128)(2,1)S(1)} %get-tuple-element.141) | copy-start | bytes 2359300
  88.9 18.2 %copy-start.134 = (bf16[1536,768]{1,0:T(8,128)(2,1)S(1)}, bf16[1536,768]{1,0:T(8,128)(2,1)}, u32[]{:S(2)}) copy-start(bf16[1536,768]{1,0:T(8,128)(2,1)} %param.54) | copy-start | bytes 7077892
  110.9 3.8 collective-permute-start.4
  117.7 7.1 %slice-start.11 = ((s8[6291456]{0:T(1024)(128)(4,1)}), s8[4194304]{0:T(1024)(128)(4,1)S(1)}, s32[]{:S(2)}) async-start(s8[6291456]{0:T(1024)(128)(4,1)} %bitcast.216), calls=%async_computation.14 | async-start | bytes 8388608
  119.4 5.4 %slice-start.12 = ((s8[6291456]{0:T(1024)(128)(4,1)}), s8[2097152]{0:T(1024)(128)(4,1)S(1)}, s32[]{:S(2)}) async-start(s8[6291456]{0:T(1024)(128)(4,1)} %bitcast.216), calls=%async_computation.15 | async-start | bytes 4194304
  124.8 13.8 %copy-start.27 = (f32[1024,768]{0,1:T(8,128)}, f32[1024,768]{0,1:T(8,128)S(1)}, u32[]{:S(2)}) copy-start(f32[1024,768]{0,1:T(8,128)S(1)} %get-tuple-element.120) | copy-start | bytes 9437188
  136.2 2.4 collective-permute-start.5
  140.6 5.5 %copy-start.109 = (f32[512]{0:T(512)}, f32[512]{0:T(512)S(1)}, u32[]{:S(2)}) copy-start(f32[512]{0:T(512)S(1)} %negate_multiply_fusion.3) | copy-start | bytes 6148
  141.9 2.5 collective-permute-start.6
  148.6 11.7 %copy-start.45 = (bf16[512,384]{0,1:T(8,128)(2,1)}, bf16[512,384]{0,1:T(8,128)(2,1)S(1)}, u32[]{:S(2)}) copy-start(bf16[512,384]{0,1:T(8,128)(2,1)S(1)} %get-tuple-element.146) | copy-start | bytes 1179652
  148.6 11.7 %slice-start = ((s8[12582912]{0:T(1024)(128)(4,1)}), s8[4194304]{0:T(1024)(128)(4,1)S(1)}, s32[]{:S(2)}) async-start(s8[12582912]{0:T(1024)(128)(4,1)} %bitcast.152), calls=%async_computation.3 | async-start | bytes 8388608
  148.9 11.5 %slice-start.1 = ((s8[12582912]{0:T(1024)(128)(4,1)}), s8[4194304]{0:T(1024)(128)(4,1)S(1)}, s32[]{:S(2)}) async-start(s8[12582912]{0:T(1024)(128)(4,1)} %bitcast.152), calls=%async_computation.4 | async-start | bytes 8388608
  148.9 12.2 %slice-start.2 = ((s8[12582912]{0:T(1024)(128)(4,1)}), s8[4194304]{0:T(1024)(128)(4,1)S(1)}, s32[]{:S(2)}) async-start(s8[12582912]{0:T(1024)(128)(4,1)} %bitcast.152), calls=%async_computation.5 | async-start | bytes 8388608
  161.1 10.4 %copy-start.26 = (bf16[1024,384]{0,1:T(8,128)(2,1)S(1)}, bf16[1024,384]{0,1:T(8,128)(2,1)}, u32[]{:S(2)}) copy-start(bf16[1024,384]{0,1:T(8,128)(2,1)} %copy-done.25) | copy-start | bytes 2359300
  161.1 19.6 %slice-start.3 = ((s8[12582912]{0:T(1024)(128)(4,1)}), s8[4194304]{0:T(1024)(128)(4,1)S(1)}, s32[]{:S(2)}) async-start(s8[12582912]{0:T(1024)(128)(4,1)} %bitcast.154), calls=%async_computation.6 | async-start | bytes 8388608
  161.1 19.6 %slice-start.4 = ((s8[12582912]{0:T(1024)(128)(4,1)}), s8[4194304]{0:T(1024)(128)(4,1)S(1)}, s32[]{:S(2)}) async-start(s8[12582912]{0:T(1024)(128)(4,1)} %bitcast.154), calls=%async_computation.7 | async-start | bytes 8388608
  171.5 9.2 %slice-start.5 = ((s8[12582912]{0:T(1024)(128)(4,1)}), s8[4194304]{0:T(1024)(128)(4,1)S(1)}, s32[]{:S(2)}) async-start(s8[12582912]{0:T(1024)(128)(4,1)} %bitcast.154), calls=%async_computation.8 | async-start | bytes 8388608
  176.5 26.4 %copy-start.66 = (bf16[6,64,512]{2,1,0:T(8,128)(2,1)}, bf16[6,64,512]{2,1,0:T(8,128)(2,1)S(1)}, u32[]{:S(2)}) copy-start(bf16[6,64,512]{2,1,0:T(8,128)(2,1)S(1)} %convolution_convert_fusion.17) | copy-start | bytes 1179652
  227.6 5.3 %copy-start.56 = (bf16[512,768]{0,1:T(8,128)(2,1)S(1)}, bf16[512,768]{0,1:T(8,128)(2,1)}, u32[]{:S(2)}) copy-start(bf16[512,768]{0,1:T(8,128)(2,1)} %copy-done.55) | copy-start | bytes 2359300
  227.6 5.3 %copy-start.58 = (bf16[512,768]{0,1:T(8,128)(2,1)S(1)}, bf16[512,768]{0,1:T(8,128)(2,1)}, u32[]{:S(2)}) copy-start(bf16[512,768]{0,1:T(8,128)(2,1)} %copy-done.57) | copy-start | bytes 2359300
  227.6 5.3 %copy-start.144 = (bf16[1024,1536]{1,0:T(8,128)(2,1)S(1)}, bf16[1024,1536]{1,0:T(8,128)(2,1)}, u32[]{:S(2)}) copy-start(bf16[1024,1536]{1,0:T(8,128)(2,1)} %copy-done.143) | copy-start | bytes 9437188
  227.7 9.1 %collective-permute-start.7 = (bf16[512,768]{0,1:T(8,128)(2,1)S(1)}, bf16[512,768]{0,1:T(8,128)(2,1)S(1)}, u32[]{:S(2)}, u32[]{:S(2)}) collective-permute-start(bf16[512,768]{0,1:T(8,128)(2,1)S(1)} %broadcast_select_fusion.4), channel_id=1, source_target_pairs={{0,1},{1,0},{2,3},{3,2},{4,5},{5,4},{6,7},{7,6},{8,9},{9,8},{10,11... | collective-permute-start | bytes 2359304 | tf_op jit(solution)/shard_map/ppermute | solution.py:151
  239.0 7.3 %copy-start.107 = (f32[512]{0:T(512)}, f32[512]{0:T(512)S(1)}, u32[]{:S(2)}) copy-start(f32[512]{0:T(512)S(1)} %negate_multiply_fusion.2) | copy-start | bytes 6148
  241.2 11.7 %collective-permute-start.8 = (bf16[512,768]{0,1:T(8,128)(2,1)}, bf16[512,768]{0,1:T(8,128)(2,1)}, u32[]{:S(2)}, u32[]{:S(2)}) collective-permute-start(bf16[512,768]{0,1:T(8,128)(2,1)} %add_convert_fusion.11), channel_id=1, source_target_pairs={{0,1},{1,0},{2,3},{3,2},{4,5},{5,4},{6,7},{7,6},{8,9},{9,8},{10,11... | collective-permute-start | bytes 2359304 | tf_op jit(solution)/shard_map/ppermute | solution.py:151
  246.3 6.6 %copy-start.14 = (f32[512,768]{0,1:T(8,128)S(1)}, f32[512,768]{0,1:T(8,128)}, u32[]{:S(2)}) copy-start(f32[512,768]{0,1:T(8,128)} %copy-done.13) | copy-start | bytes 4718596
  252.5 89.6 %collective-permute-start.11 = (f32[3072]{0:T(1024)}, f32[3072]{0:T(1024)}, u32[]{:S(2)}, u32[]{:S(2)}) collective-permute-start(f32[3072]{0:T(1024)} %pad_maximum_fusion.15), channel_id=1, source_target_pairs={{0,1},{1,0},{2,3},{3,2},{4,5},{5,4},{6,7},{7,6},{8,9},{9,8},{10,11... | collective-permute-start | bytes 36872 | tf_op jit(solution)/shard_map/ppermute | solution.py:151
  257.7 16.5 %copy-start.47 = (bf16[512,384]{0,1:T(8,128)(2,1)}, bf16[512,384]{0,1:T(8,128)(2,1)S(1)}, u32[]{:S(2)}) copy-start(bf16[512,384]{0,1:T(8,128)(2,1)S(1)} %get-tuple-element.144) | copy-start | bytes 1179652
  257.9 6.4 %copy-start.50 = (bf16[1024,384]{0,1:T(8,128)(2,1)S(1)}, bf16[1024,384]{0,1:T(8,128)(2,1)}, u32[]{:S(2)}) copy-start(bf16[1024,384]{0,1:T(8,128)(2,1)} %copy-done.49) | copy-start | bytes 2359300
  257.9 16.3 %slice-start.6 = ((s8[12582912]{0:T(1024)(128)(4,1)}), s8[4194304]{0:T(1024)(128)(4,1)S(1)}, s32[]{:S(2)}) async-start(s8[12582912]{0:T(1024)(128)(4,1)} %bitcast.156), calls=%async_computation.9 | async-start | bytes 8388608
  257.9 16.3 %slice-start.7 = ((s8[12582912]{0:T(1024)(128)(4,1)}), s8[4194304]{0:T(1024)(128)(4,1)S(1)}, s32[]{:S(2)}) async-start(s8[12582912]{0:T(1024)(128)(4,1)} %bitcast.156), calls=%async_computation.10 | async-start | bytes 8388608
  264.4 9.8 %slice-start.8 = ((s8[12582912]{0:T(1024)(128)(4,1)}), s8[4194304]{0:T(1024)(128)(4,1)S(1)}, s32[]{:S(2)}) async-start(s8[12582912]{0:T(1024)(128)(4,1)} %bitcast.156), calls=%async_computation.11 | async-start | bytes 8388608
  264.4 9.8 %copy-start.18 = (pred[512,1024]{1,0:T(8,128)(4,1)S(1)}, pred[512,1024]{1,0:T(8,128)(4,1)}, u32[]{:S(2)}) copy-start(pred[512,1024]{1,0:T(8,128)(4,1)} %copy-done.17) | copy-start | bytes 1572868
  281.4 19.2 %copy-start.24 = (bf16[1024,384]{0,1:T(8,128)(2,1)S(1)}, bf16[1024,384]{0,1:T(8,128)(2,1)}, u32[]{:S(2)}) copy-start(bf16[1024,384]{0,1:T(8,128)(2,1)} %copy-done.23) | copy-start | bytes 2359300
  300.6 10.5 %slice-start.9 = ((s8[6291456]{0:T(1024)(128)(4,1)}), s8[4194304]{0:T(1024)(128)(4,1)S(1)}, s32[]{:S(2)}) async-start(s8[6291456]{0:T(1024)(128)(4,1)} %bitcast.158), calls=%async_computation.12 | async-start | bytes 8388608
  305.7 5.4 %slice-start.10 = ((s8[6291456]{0:T(1024)(128)(4,1)}), s8[2097152]{0:T(1024)(128)(4,1)S(1)}, s32[]{:S(2)}) async-start(s8[6291456]{0:T(1024)(128)(4,1)} %bitcast.158), calls=%async_computation.13 | async-start | bytes 4194304
  313.2 6.5 %copy-start.43 = (bf16[6,64,512]{2,1,0:T(8,128)(2,1)}, bf16[6,64,512]{2,1,0:T(8,128)(2,1)S(1)}, u32[]{:S(2)}) copy-start(bf16[6,64,512]{2,1,0:T(8,128)(2,1)S(1)} %convolution_convert_fusion.14) | copy-start | bytes 1179652
  322.3 5.6 %copy-start.88 = (bf16[1024,768]{1,0:T(8,128)(2,1)S(1)}, bf16[1024,768]{1,0:T(8,128)(2,1)}, u32[]{:S(2)}) copy-start(bf16[1024,768]{1,0:T(8,128)(2,1)} %param.28) | copy-start | bytes 4718596
  337.7 5.3 %copy-start.113 = (f32[768]{0:T(1024)S(1)}, f32[768]{0:T(1024)}, u32[]{:S(2)}) copy-start(f32[768]{0:T(1024)} %get-tuple-element.119) | copy-start | bytes 9220
  358.0 143.9 %all-to-all-start = ((f32[16,1,83712]{2,1,0:T(1,128)}), f32[16,1,83712]{2,1,0:T(1,128)}, u32[]{:S(2)}, u32[]{:S(2)}) async-start(f32[16,1,83712]{2,1,0:T(1,128)} %copy.104), calls=%async_computation | async-start | bytes 10715136 | tf_op jit(solution)/shard_map/all_to_all | solution.py:345
  368.7 8.1 %collective-permute-start.10 = (bf16[512,768]{0,1:T(8,128)(2,1)S(1)}, bf16[512,768]{0,1:T(8,128)(2,1)}, u32[]{:S(2)}, u32[]{:S(2)}) collective-permute-start(bf16[512,768]{0,1:T(8,128)(2,1)S(1)} %broadcast_select_fusion), channel_id=1, source_target_pairs={{0,1},{1,0},{2,3},{3,2},{4,5},{5,4},{6,7},{7,6},{8,9},{9,8},{10,11... | collective-permute-start | bytes 2359304 | tf_op jit(solution)/shard_map/ppermute | solution.py:151
  374.1 8.8 %collective-permute-start.9 = (bf16[512,768]{0,1:T(8,128)(2,1)S(1)}, bf16[512,768]{0,1:T(8,128)(2,1)}, u32[]{:S(2)}, u32[]{:S(2)}) collective-permute-start(bf16[512,768]{0,1:T(8,128)(2,1)S(1)} %broadcast_select_fusion.1), channel_id=1, source_target_pairs={{0,1},{1,0},{2,3},{3,2},{4,5},{5,4},{6,7},{7,6},{8,9},{9,8},{10,11... | collective-permute-start | bytes 2359304 | tf_op jit(solution)/shard_map/ppermute | solution.py:151
  376.8 6.1 %copy-start.108 = (f32[512]{0:T(512)S(1)}, f32[512]{0:T(512)}, u32[]{:S(2)}) copy-start(f32[512]{0:T(512)} %copy-done.107) | copy-start | bytes 6148
  501.9 13.6 %copy-start.1 = (bf16[768,1536]{1,0:T(8,128)(2,1)S(1)}, bf16[768,1536]{1,0:T(8,128)(2,1)}, u32[]{:S(2)}) copy-start(bf16[768,1536]{1,0:T(8,128)(2,1)} %param.52) | copy-start | bytes 7077892
  (108 other events, 293.4 us)
Sparse Core Ops, SparseCore 0:
  246.4 217.9 reduce-scatter.1
